TPU v7x, 32 devices: a whole 2x2x4 slice. The times are simulated.
32 devices in a mesh: freq: 4 (over y, x), param: 8 (over z, core).
Axes of the slice: x: 2, y: 2, z: 4, core: 2. Of those that a mesh axis runs over, the one named last changes fastest.
Arguments:
- sources: float32 [4, 420, 1024], P(None, None, ('param', 'freq')), may hold values from -6 to 6
- kernel: bfloat16 [424, 2, 600, 1024], P('freq', None, None, 'param'), may hold values from -0.125 to 0.125
- bin_of_slot: int32 [424], replicated, may hold values from 0 to 420, as said below
Outputs:
- observations: float32 [4, 420, 600], P(None, None, 'freq')
Inputs may be any that keep to these rules, and one draw needn't show every extreme that they name: `bin_of_slot`: every bin from 0 to 420 is named by at least one slot; the other slots name bins again.
All inputs are finite; a program needn't handle non-finite values.
Results may differ from a plain program's by a relative error of at most 0.0031.
Values may be sent and summed in bfloat16 or wider, within the bound.
No kernel may reach another device: no remote copies, remote signals or barrier semaphores. Data moves between devices by JAX's collectives and lax.ppermute only.
A program may use at most 128 MiB of HBM per device.

v0:
```python
import functools
import math

import jax
import jax.numpy as jnp
import numpy as np
from jax import lax
from jax.experimental import pallas as pl
from jax.experimental.pallas import tpu as pltpu
from jax.sharding import PartitionSpec as P

LANES = 128
BF16, F32, I32 = jnp.bfloat16, jnp.float32, jnp.int32
VMEM = pltpu.VMEM
CHUNK = 8


def up(value, unit):
    return -(-value // unit) * unit


def dot_nt(left, right):
    return lax.dot_general(left, right, (((1,), (1,)), ((), ())), preferred_element_type=F32)


def dot_nn(left, right):
    return jnp.dot(left, right, preferred_element_type=F32)


def halves(value):
    high = value.astype(BF16)
    return high, (value - high.astype(F32)).astype(BF16)


class Plan:
    def __init__(self, mesh, sources, kernel, bin_of_slot):
        self.freq = mesh.shape["freq"]
        self.param = mesh.shape["param"]
        self.pieces = self.param // 2
        self.count, self.steps, self.mine = sources.shape
        self.slots = bin_of_slot.shape[0]
        self.here, _, self.sensors, self.depth = kernel.shape
        self.half = self.count // 2
        self.comps = 2 * self.half
        self.group = LANES // self.comps
        self.groups = -(-self.here // self.group)
        self.block = self.sensors // self.freq
        self.block_pad = up(self.block, 8)
        self.bins = up(self.steps + 1, LANES)
        self.span = -(-self.steps // self.pieces)
        self.span_pad = up(self.span, LANES)
        self.slots_pad = up(self.slots, LANES)
        assert self.here <= LANES and self.depth == self.mine * self.freq
        assert self.freq & (self.freq - 1) == 0 and self.pieces & (self.pieces - 1) == 0

    def tables(self):
        times = np.arange(self.steps)
        rows = times // self.span * self.span_pad + times % self.span
        bins = np.arange(self.steps + 1)
        angle = (times[:, None] * bins[None, :] % (2 * self.steps)) * (math.pi / self.steps)
        table = np.zeros((self.pieces * self.span_pad, 2 * self.bins), np.float64)
        table[rows, : self.steps + 1] = np.cos(angle)
        table[rows, self.bins : self.bins + self.steps + 1] = np.sin(angle)
        high = table.astype(jnp.bfloat16)
        low = (table - high.astype(np.float64)).astype(jnp.bfloat16)
        return high, low


def bin_row(plan, bins_ref, row_ref):
    row_ref[...] = jnp.full(row_ref.shape, -1, I32)
    row_ref[0:1, 0 : plan.slots] = bins_ref[...]
    return row_ref[0:1, :]


def slot_hits(plan, row, shard):
    shift = (-plan.here * shard) % plan.slots_pad
    if shift:
        row = pltpu.roll(row, shift, 1)
    row = row[:, :LANES]
    lane = lax.broadcasted_iota(I32, (1, LANES), 1)
    row = jnp.where(lane < plan.here, row, -1)
    bins = lax.broadcasted_iota(I32, (plan.bins, LANES), 0)
    return jnp.where(bins == row, 1.0, 0.0).astype(BF16)


def forward_kernel(plan, bins_ref, src_ref, high_ref, low_ref, *rest):
    outs, (row_ref, time_ref, send_ref) = rest[: plan.freq], rest[plan.freq :]
    me = lax.axis_index("freq")
    time_ref[...] = jnp.zeros(time_ref.shape, F32)
    for c in range(plan.count):
        for z in range(plan.pieces):
            first = z * plan.span
            size = min(plan.span, plan.steps - first)
            time_ref[
                z * plan.span_pad : z * plan.span_pad + size, c * plan.mine : (c + 1) * plan.mine
            ] = src_ref[c, first : first + size, :]
    rows = plan.count * plan.mine
    high, low = halves(time_ref[...].T[:rows])
    spectrum = (
        dot_nn(high, high_ref[...]) + dot_nn(high, low_ref[...]) + dot_nn(low, high_ref[...])
    )
    scale = 1.0 / math.sqrt(plan.steps)
    both = jnp.concatenate(
        [
            (spectrum[:, : plan.bins] * scale).astype(BF16),
            (spectrum[:, plan.bins :] * -scale).astype(BF16),
        ],
        axis=0,
    )
    row = bin_row(plan, bins_ref, row_ref)
    for shard in range(plan.freq):
        picked = dot_nn(both, slot_hits(plan, row, shard))
        for c in range(plan.count):
            for part in range(2):
                first = part * rows + c * plan.mine
                comp = 2 * (c % plan.half) + part
                value = picked[first : first + plan.mine]
                if comp:
                    value = pltpu.roll(value, comp * plan.group, 1)
                send_ref[shard, 2 * c + part] = value.astype(BF16)
    for k in range(plan.freq):
        outs[k][...] = send_ref[me ^ k]


def response_kernel(plan, first_group, last_group, *refs):
    freq, group = plan.freq, plan.group
    arrived, kern_ref = refs[:freq], refs[freq]
    own_ref, other_ref, buf_ref, spec_ref, rhs_ref, acc_ref, sem_ref = refs[freq + 1 :]
    first = first_group * group
    total = min(last_group * group, plan.here) - first
    chunks = [(at, min(CHUNK, total - at)) for at in range(0, total, CHUNK)]
    copies = [
        pltpu.make_async_copy(
            kern_ref.at[pl.ds(first + at, size)], buf_ref.at[pl.ds(at, size)], sem_ref.at[i]
        )
        for i, (at, size) in enumerate(chunks)
    ]
    for copy in copies:
        copy.start()
    me, core = lax.axis_index("freq"), lax.axis_index("param") % 2
    for k in range(freq):
        at = pl.multiple_of((me ^ k) * plan.mine, plan.mine)
        spec_ref[:, pl.ds(at, plan.mine), :] = arrived[k][...]
    lane = lax.broadcasted_iota(I32, (plan.depth, LANES), 1)
    for g in range(first_group, last_group):
        for side in range(2):
            base = (core ^ side) * plan.comps
            place = (lane // group - g) % plan.comps
            real = spec_ref[base].astype(F32)
            for comp in range(1, plan.comps):
                real = jnp.where(place == comp, spec_ref[base + comp].astype(F32), real)
            imag = jnp.where(
                place % 2 == 0, -pltpu.roll(real, LANES - group, 1), pltpu.roll(real, group, 1)
            )
            cols = slice(side * LANES, (side + 1) * LANES)
            rhs_ref[g - first_group, : plan.depth, cols] = real.astype(BF16)
            rhs_ref[g - first_group, plan.depth :, cols] = imag.astype(BF16)
    within = lax.broadcasted_iota(I32, (2 * plan.depth, 2 * LANES), 1) % group

    def product(g, at, size):
        weights = rhs_ref[g]
        left, right = [], []
        for s in range(size):
            left += [buf_ref[at + s, 0], buf_ref[at + s, 1]]
            right.append(jnp.where(within == (at + s) % group, weights, jnp.zeros_like(weights)))
        return dot_nn(jnp.concatenate(left, axis=1), jnp.concatenate(right, axis=0))

    for g in range(last_group - first_group):
        inside = [(i, at, size) for i, (at, size) in enumerate(chunks) if at // group == g]
        for n, (i, at, size) in enumerate(inside):
            copies[i].wait()
            value = product(g, at, size)
            if n:
                value = acc_ref[...] + value
            if n + 1 < len(inside):
                acc_ref[...] = value
        for f in range(freq):
            rows = value[f * plan.block : (f + 1) * plan.block]
            own_ref[f, g] = rows[:, :LANES]
            other_ref[f, g] = rows[:, LANES:]


def join_kernel(plan, own_ref, other_ref, *outs):
    me = lax.axis_index("freq")
    for k in range(plan.freq):
        outs[k][...] = (own_ref[me ^ k] + other_ref[me ^ k]).astype(BF16)


def inverse_kernel(plan, calls, bins_ref, high_ref, low_ref, *rest):
    freq, group, pad = plan.freq, plan.group, plan.block_pad
    arrived, rest = rest[: calls * freq], rest[calls * freq :]
    outs, (row_ref, hits_ref, joined_ref) = rest[: plan.pieces], rest[plan.pieces :]
    me, piece = lax.axis_index("freq"), lax.axis_index("param") // 2
    row = bin_row(plan, bins_ref, row_ref)
    for shard in range(freq):
        hits_ref[shard] = slot_hits(plan, row, shard)
    lane = lax.broadcasted_iota(I32, (plan.block, LANES), 1)
    joined_ref[...] = jnp.zeros(joined_ref.shape, BF16)
    for k in range(freq):
        tiles = []
        for call in range(calls):
            ref = arrived[call * freq + k]
            tiles += [ref[g].astype(F32) for g in range(ref.shape[0])]
        for comp in range(plan.comps):
            value = jnp.zeros((plan.block, LANES), F32)
            for g, tile in enumerate(tiles):
                value = jnp.where(lane // group == (g + comp) % plan.comps, tile, value)
            if comp:
                value = pltpu.roll(value, LANES - comp * group, 1)
            at = comp * pad
            joined_ref[at : at + plan.block, k * LANES : (k + 1) * LANES] = value.astype(BF16)
    hits = jnp.concatenate([hits_ref[me ^ k] for k in range(freq)], axis=1)
    by_bin = dot_nt(joined_ref[...], hits)
    bins = lax.broadcasted_iota(I32, (1, plan.bins), 1)
    weight = jnp.where((bins == 0) | (bins == plan.steps), 1.0, 2.0) * (
        1.0 / math.sqrt(2.0 * (plan.steps + 1))
    )
    rows = []
    for c in range(plan.half):
        real = by_bin[2 * c * pad : (2 * c + 1) * pad] * weight
        imag = by_bin[(2 * c + 1) * pad : (2 * c + 2) * pad] * -weight
        rows.append(jnp.concatenate([real, imag], axis=1))
    high, low = halves(jnp.concatenate(rows, axis=0))
    for k in range(plan.pieces):
        at = pl.multiple_of((piece ^ k) * plan.span_pad, plan.span_pad)
        table_high = high_ref[pl.ds(at, plan.span_pad), :]
        table_low = low_ref[pl.ds(at, plan.span_pad), :]
        value = dot_nt(high, table_high) + dot_nt(low, table_high) + dot_nt(high, table_low)
        outs[k][...] = value.astype(outs[k].dtype)


def sum_kernel(*refs):
    value = refs[0][...]
    for ref in refs[1:-1]:
        value = value + ref[...].astype(F32)
    refs[-1][...] = value.astype(BF16)


def output_kernel(plan, *refs):
    out_ref = refs[-1]
    piece, core = lax.axis_index("param") // 2, lax.axis_index("param") % 2
    width = plan.span_pad
    time = lax.broadcasted_iota(I32, (plan.steps, plan.pieces * width), 0)
    lane = lax.broadcasted_iota(I32, (plan.steps, plan.pieces * width), 1)
    inside = lane % width
    target = (lane // width ^ piece) * plan.span + inside
    pick = jnp.where((time == target) & (inside < plan.span), 1.0, 0.0).astype(BF16)
    for side in range(2):
        parts = refs[side * plan.pieces : (side + 1) * plan.pieces]
        for c in range(plan.half):
            at = c * plan.block_pad
            value = jnp.concatenate([ref[at : at + plan.block_pad, :] for ref in parts], axis=1)
            out_ref[(core ^ side) * plan.half + c] = dot_nt(pick, value)[:, : plan.block]


def call(body, out_shapes, args, in_specs=None, scratch=(), cost=None, limit=None):
    whole = pl.BlockSpec(memory_space=VMEM)
    return pl.pallas_call(
        body,
        out_shape=out_shapes,
        in_specs=in_specs or [whole] * len(args),
        out_specs=jax.tree.map(lambda _: whole, out_shapes),
        scratch_shapes=list(scratch),
        cost_estimate=cost,
        compiler_params=pltpu.CompilerParams(vmem_limit_bytes=limit),
    )(*args)


def shards(mesh, sources, kernel, bin_of_slot):
    plan = Plan(mesh, sources, kernel, bin_of_slot)
    freq, pieces = plan.freq, plan.pieces
    shape = jax.ShapeDtypeStruct
    high, low = plan.tables()
    bins = bin_of_slot.reshape(1, plan.slots)
    row = VMEM((8, plan.slots_pad), I32)
    whole = pl.BlockSpec(memory_space=VMEM)

    def over_freq(values):
        return [values[0]] + [
            lax.ppermute(values[k], "freq", [(i, i ^ k) for i in range(freq)])
            for k in range(1, freq)
        ]

    def to_piece(value, k):
        pairs = [(2 * z + h, 2 * (z ^ k) + h) for z in range(pieces) for h in range(2)]
        return lax.ppermute(value, "param", pairs)

    def to_core(value):
        return lax.ppermute(value, "param", [(i, i ^ 1) for i in range(plan.param)])

    spectra = call(
        functools.partial(forward_kernel, plan),
        [shape((2 * plan.count, plan.mine, LANES), BF16)] * freq,
        (bins, sources, high, low),
        scratch=[
            row,
            VMEM((pieces * plan.span_pad, up(plan.count * plan.mine, LANES)), F32),
            VMEM((freq, 2 * plan.count, plan.mine, LANES), BF16),
        ],
    )
    arrived = over_freq(spectra)

    middle = -(-plan.groups // 2)
    ranges = [(0, middle), (middle, plan.groups)]
    parts = []
    for begin, end in ranges:
        total = min(end * plan.group, plan.here) - begin * plan.group
        size = shape((freq, end - begin, plan.block, LANES), F32)
        own, other = call(
            functools.partial(response_kernel, plan, begin, end),
            [size, size],
            (*arrived, kernel),
            in_specs=[whole] * freq + [pl.BlockSpec(memory_space=pl.ANY)],
            scratch=[
                VMEM((total, 2, plan.sensors, plan.depth), BF16),
                VMEM((2 * plan.count, plan.depth, LANES), BF16),
                VMEM((end - begin, 2 * plan.depth, 2 * LANES), BF16),
                VMEM((plan.sensors, 2 * LANES), F32),
                pltpu.SemaphoreType.DMA((-(-total // CHUNK),)),
            ],
            cost=pl.CostEstimate(
                flops=total * 2 * plan.sensors * plan.depth * 256,
                bytes_accessed=total * 4 * plan.sensors * plan.depth,
                transcendentals=0,
            ),
            limit=56 * 1024 * 1024,
        )
        summed = call(
            functools.partial(join_kernel, plan),
            [shape((end - begin, plan.block, LANES), BF16)] * freq,
            (own, to_core(other)),
        )
        parts += over_freq(summed)

    rows = plan.half * plan.block_pad
    partial = call(
        functools.partial(inverse_kernel, plan, len(ranges)),
        [shape((rows, plan.span_pad), BF16 if k else F32) for k in range(pieces)],
        (bins, high, low, *parts),
        scratch=[
            row,
            VMEM((freq, plan.bins, LANES), BF16),
            VMEM((plan.comps * plan.block_pad, freq * LANES), BF16),
        ],
    )
    received = [to_piece(partial[k], k) for k in range(1, pieces)]
    piece = call(sum_kernel, shape((rows, plan.span_pad), BF16), (partial[0], *received))
    mine = [piece] + [to_piece(piece, k) for k in range(1, pieces)]
    theirs = [to_core(value) for value in mine]
    return call(
        functools.partial(output_kernel, plan),
        shape((plan.count, plan.steps, plan.block), F32),
        (*mine, *theirs),
    )


def solution(mesh):
    return jax.shard_map(
        functools.partial(shards, mesh),
        mesh=mesh,
        in_specs=(P(None, None, ("param", "freq")), P("freq", None, None, "param"), P()),
        out_specs=P(None, None, "freq"),
        check_vma=False,
    )
```

profile of v0, /device:TPU:0, one launch (start us, length us, event | category | flops | bytes accessed | tf_op | source)
XLA Modules:
  0.0 95.6 jit_solution(16394066364749184627)
XLA Ops:
  0.0 2.2 %copy.8.src_ref = f32[4,420,32]{2,1,0:T(8,128)} copy(f32[4,420,32]{1,2,0:T(8,128)} %param.5) | data formatting | bytes 430080 | tf_op args[0]
  2.2 3.8 %shard_map.55 = (bf16[8,32,128]{2,1,0:T(8,128)(2,1)}, bf16[8,32,128]{2,1,0:T(8,128)(2,1)}, bf16[8,32,128]{2,1,0:T(8,128)(2,1)}, bf16[8,32,128]{2,1,0:T(8,128)(2,1)}) custom-call(s32[1,424]{1,0:T(1,128)} %bitcast.1, f32[4,420,32]{2,1,0:T(8,128)} %copy.8.src_ref, bf16[512,1024]{1,0:T(8,128)(2,1)} %constant.4.clone.high_ref, ...), custom_call_target="tpu_custom_call" | custom-call | tf_op jit(solution)/shard_map/pallas_call | solution.py:258
  5.9 3.0 %collective-permute-start = (bf16[8,32,128]{2,1,0:T(8,128)(2,1)}, bf16[8,32,128]{2,1,0:T(8,128)(2,1)S(1)}, u32[]{:S(2)}, u32[]{:S(2)}) collective-permute-start(bf16[8,32,128]{2,1,0:T(8,128)(2,1)} %get-tuple-element.26), channel_id=1, source_target_pairs={{0,8},{8,0},{16,24},{24,16},{1,9},{9,1},{17,25},{25,17},{2,10},{10... | collective-permute-start | bytes 196616 | tf_op jit(solution)/shard_map/ppermute | solution.py:280
  8.9 1.5 %collective-permute-start.1 = (bf16[8,32,128]{2,1,0:T(8,128)(2,1)}, bf16[8,32,128]{2,1,0:T(8,128)(2,1)S(1)}, u32[]{:S(2)}, u32[]{:S(2)}) collective-permute-start(bf16[8,32,128]{2,1,0:T(8,128)(2,1)} %get-tuple-element.27), channel_id=1, source_target_pairs={{0,16},{8,24},{16,0},{24,8},{1,17},{9,25},{17,1},{25,9},{2,18},{10... | collective-permute-start | bytes 196616 | tf_op jit(solution)/shard_map/ppermute | solution.py:280
  11.6 1.8 %collective-permute-done.1.refs_2_ = bf16[8,32,128]{2,1,0:T(8,128)(2,1)S(1)} collective-permute-done((bf16[8,32,128]{2,1,0:T(8,128)(2,1)}, bf16[8,32,128]{2,1,0:T(8,128)(2,1)S(1)}, u32[]{:S(2)}, u32[]{:S(2)}) %collective-permute-start.1) | collective-permute-done | bytes 65568 | tf_op jit(solution)/shard_map/ppermute | solution.py:280
  13.4 2.4 %collective-permute-done.2.refs_3_ = bf16[8,32,128]{2,1,0:T(8,128)(2,1)S(1)} collective-permute-done((bf16[8,32,128]{2,1,0:T(8,128)(2,1)}, bf16[8,32,128]{2,1,0:T(8,128)(2,1)S(1)}, u32[]{:S(2)}, u32[]{:S(2)}) %collective-permute-start.2) | collective-permute-done | bytes 65568 | tf_op jit(solution)/shard_map/ppermute | solution.py:280
  16.4 10.4 %shard_map.58 = (f32[4,2,150,128]{3,2,1,0:T(8,128)}, f32[4,2,150,128]{3,2,1,0:T(8,128)}) custom-call(bf16[8,32,128]{2,1,0:T(8,128)(2,1)} %get-tuple-element.25.refs_0_, bf16[8,32,128]{2,1,0:T(8,128)(2,1)} %copy-done, bf16[8,32,128]{2,1,0:T(8,128)(2,1)} %copy-done.1, bf16[8,32,128]{2,1,0:T(8,128)(2,1)} %copy-done.2, bf16[106,2,600,128]{3,2,1,0:T(8,128)(2,1)} %refs_4_.3), custom_call_target="tpu_custom_call" | custom-call | flops 1651507200 | bytes 12902400 | tf_op jit(solution)/shard_map/pallas_call | solution.py:258
  28.3 14.5 %shard_map.56 = (f32[4,2,150,128]{3,2,1,0:T(8,128)}, f32[4,2,150,128]{3,2,1,0:T(8,128)}) custom-call(bf16[8,32,128]{2,1,0:T(8,128)(2,1)} %get-tuple-element.25.refs_0_, bf16[8,32,128]{2,1,0:T(8,128)(2,1)} %copy-done, bf16[8,32,128]{2,1,0:T(8,128)(2,1)} %copy-done.1, bf16[8,32,128]{2,1,0:T(8,128)(2,1)} %copy-done.2, bf16[106,2,600,128]{3,2,1,0:T(8,128)(2,1)} %refs_4_.3), custom_call_target="tpu_custom_call" | custom-call | flops 2516582400 | bytes 19660800 | tf_op jit(solution)/shard_map/pallas_call | solution.py:258
  45.6 2.0 %shard_map.59 = (bf16[2,150,128]{2,1,0:T(8,128)(2,1)}, bf16[2,150,128]{2,1,0:T(8,128)(2,1)}, bf16[2,150,128]{2,1,0:T(8,128)(2,1)}, bf16[2,150,128]{2,1,0:T(8,128)(2,1)}) custom-call(f32[4,2,150,128]{3,2,1,0:T(8,128)} %get-tuple-element.35.own_ref, f32[4,2,150,128]{3,2,1,0:T(8,128)} %copy.12.other_ref), custom_call_target="tpu_custom_call" | custom-call | tf_op jit(solution)/shard_map/pallas_call | solution.py:258
  48.5 2.7 %collective-permute-start.10 = (bf16[2,150,128]{2,1,0:T(8,128)(2,1)}, bf16[2,150,128]{2,1,0:T(8,128)(2,1)S(1)}, u32[]{:S(2)}, u32[]{:S(2)}) collective-permute-start(bf16[2,150,128]{2,1,0:T(8,128)(2,1)} %get-tuple-element.40), channel_id=1, source_target_pairs={{0,24},{8,16},{16,8},{24,0},{1,25},{9,17},{17,9},{25,1},{2,26},{10... | collective-permute-start | bytes 230408 | tf_op jit(solution)/shard_map/ppermute | solution.py:280
  52.0 2.0 %shard_map.57 = (bf16[2,150,128]{2,1,0:T(8,128)(2,1)}, bf16[2,150,128]{2,1,0:T(8,128)(2,1)}, bf16[2,150,128]{2,1,0:T(8,128)(2,1)}, bf16[2,150,128]{2,1,0:T(8,128)(2,1)}) custom-call(f32[4,2,150,128]{3,2,1,0:T(8,128)} %get-tuple-element.29.own_ref, f32[4,2,150,128]{3,2,1,0:T(8,128)} %copy.10.other_ref), custom_call_target="tpu_custom_call" | custom-call | tf_op jit(solution)/shard_map/pallas_call | solution.py:258
  54.9 2.7 %collective-permute-start.6 = (bf16[2,150,128]{2,1,0:T(8,128)(2,1)}, bf16[2,150,128]{2,1,0:T(8,128)(2,1)S(1)}, u32[]{:S(2)}, u32[]{:S(2)}) collective-permute-start(bf16[2,150,128]{2,1,0:T(8,128)(2,1)} %get-tuple-element.34), channel_id=1, source_target_pairs={{0,24},{8,16},{16,8},{24,0},{1,25},{9,17},{17,9},{25,1},{2,26},{10... | collective-permute-start | bytes 230408 | tf_op jit(solution)/shard_map/ppermute | solution.py:280
  57.6 1.6 %collective-permute-done.4.rest_1_ = bf16[2,150,128]{2,1,0:T(8,128)(2,1)S(1)} collective-permute-done((bf16[2,150,128]{2,1,0:T(8,128)(2,1)}, bf16[2,150,128]{2,1,0:T(8,128)(2,1)S(1)}, u32[]{:S(2)}, u32[]{:S(2)}) %collective-permute-start.4) | collective-permute-done | bytes 76832 | tf_op jit(solution)/shard_map/ppermute | solution.py:280
  61.0 5.1 %shard_map.60 = (f32[304,128]{1,0:T(8,128)}, bf16[304,128]{1,0:T(8,128)(2,1)}, bf16[304,128]{1,0:T(8,128)(2,1)}, bf16[304,128]{1,0:T(8,128)(2,1)}) custom-call(s32[1,424]{1,0:T(1,128)} %bitcast.2, bf16[512,1024]{1,0:T(8,128)(2,1)} %constant.4.clone.high_ref, bf16[512,1024]{1,0:T(8,128)(2,1)} %constant.5.clone.low_ref, ...), custom_call_target="tpu_custom_call" | custom-call | tf_op jit(solution)/shard_map/pallas_call | solution.py:258
  66.2 1.8 %collective-permute-start.11 = (bf16[304,128]{1,0:T(8,128)(2,1)}, bf16[304,128]{1,0:T(8,128)(2,1)S(1)}, u32[]{:S(2)}, u32[]{:S(2)}) collective-permute-start(bf16[304,128]{1,0:T(8,128)(2,1)} %get-tuple-element.42), channel_id=1, source_target_pairs={{0,2},{1,3},{2,0},{3,1},{4,6},{5,7},{6,4},{7,5},{8,10},{9,11},{10,... | collective-permute-start | bytes 233480 | tf_op jit(solution)/shard_map/ppermute | solution.py:286
  67.9 2.6 %collective-permute-start.12 = (bf16[304,128]{1,0:T(8,128)(2,1)}, bf16[304,128]{1,0:T(8,128)(2,1)S(1)}, u32[]{:S(2)}, u32[]{:S(2)}) collective-permute-start(bf16[304,128]{1,0:T(8,128)(2,1)} %get-tuple-element.43), channel_id=1, source_target_pairs={{0,4},{1,5},{2,6},{3,7},{4,0},{5,1},{6,2},{7,3},{8,12},{9,13},{10,... | collective-permute-start | bytes 233480 | tf_op jit(solution)/shard_map/ppermute | solution.py:286
  71.0 4.1 %collective-permute-done.12.refs_2_ = bf16[304,128]{1,0:T(8,128)(2,1)S(1)} collective-permute-done((bf16[304,128]{1,0:T(8,128)(2,1)}, bf16[304,128]{1,0:T(8,128)(2,1)S(1)}, u32[]{:S(2)}, u32[]{:S(2)}) %collective-permute-start.12) | collective-permute-done | bytes 77856 | tf_op jit(solution)/shard_map/ppermute | solution.py:286
  75.1 1.9 %collective-permute-done.13.refs_3_ = bf16[304,128]{1,0:T(8,128)(2,1)S(1)} collective-permute-done((bf16[304,128]{1,0:T(8,128)(2,1)}, bf16[304,128]{1,0:T(8,128)(2,1)S(1)}, u32[]{:S(2)}, u32[]{:S(2)}) %collective-permute-start.13) | collective-permute-done | bytes 77856 | tf_op jit(solution)/shard_map/ppermute | solution.py:286
  77.6 1.7 %shard_map.61.refs_0_ = bf16[304,128]{1,0:T(8,128)(2,1)} custom-call(f32[304,128]{1,0:T(8,128)} %get-tuple-element.41.refs_0_, bf16[304,128]{1,0:T(8,128)(2,1)} %copy-done.16, bf16[304,128]{1,0:T(8,128)(2,1)} %copy-done.17, bf16[304,128]{1,0:T(8,128)(2,1)} %copy-done.18), custom_call_target="tpu_custom_call" | custom-call | tf_op jit(solution)/shard_map/pallas_call | solution.py:258
  80.3 3.4 %collective-permute-start.14 = (bf16[304,128]{1,0:T(8,128)(2,1)}, bf16[304,128]{1,0:T(8,128)(2,1)S(1)}, u32[]{:S(2)}, u32[]{:S(2)}) collective-permute-start(bf16[304,128]{1,0:T(8,128)(2,1)} %shard_map.61.refs_0_), channel_id=1, source_target_pairs={{0,2},{1,3},{2,0},{3,1},{4,6},{5,7},{6,4},{7,5},{8,10},{9,11},{10,... | collective-permute-start | bytes 233480 | tf_op jit(solution)/shard_map/ppermute | solution.py:286
  83.7 2.1 %collective-permute-done.16.refs_3_ = bf16[304,128]{1,0:T(8,128)(2,1)S(1)} collective-permute-done((bf16[304,128]{1,0:T(8,128)(2,1)}, bf16[304,128]{1,0:T(8,128)(2,1)S(1)}, u32[]{:S(2)}, u32[]{:S(2)}) %collective-permute-start.16) | collective-permute-done | bytes 77856 | tf_op jit(solution)/shard_map/ppermute | solution.py:286
  85.8 1.5 %collective-permute-done.15.refs_2_ = bf16[304,128]{1,0:T(8,128)(2,1)S(1)} collective-permute-done((bf16[304,128]{1,0:T(8,128)(2,1)}, bf16[304,128]{1,0:T(8,128)(2,1)S(1)}, u32[]{:S(2)}, u32[]{:S(2)}) %collective-permute-start.15) | collective-permute-done | bytes 77856 | tf_op jit(solution)/shard_map/ppermute | solution.py:286
  89.9 3.0 %shard_map.62 = f32[4,420,150]{2,1,0:T(8,128)} custom-call(bf16[304,128]{1,0:T(8,128)(2,1)} %shard_map.61.refs_0_, bf16[304,128]{1,0:T(8,128)(2,1)} %copy-done.10, bf16[304,128]{1,0:T(8,128)(2,1)} %copy-done.8, bf16[304,128]{1,0:T(8,128)(2,1)} %copy-done.6, bf16[304,128]{1,0:T(8,128)(2,1)} %copy-done.11, bf16[304,128]{1,0:T(8,128)(2,1)} %copy-done.15, ...), custom_call_target="tpu_custom_call" | custom-call | tf_op jit(solution)/shard_map/pallas_call | solution.py:258
  92.9 2.7 %copy.13 = f32[4,420,150]{1,0,2:T(4,128)} copy(f32[4,420,150]{2,1,0:T(8,128)} %shard_map.62) | data formatting | bytes 2016000 | tf_op jit(solution)/shard_map/pallas_call | solution.py:258
  (70 shorter events, 14.9 us)
Async XLA Ops:
  5.9 5.6 %collective-permute-start = (bf16[8,32,128]{2,1,0:T(8,128)(2,1)}, bf16[8,32,128]{2,1,0:T(8,128)(2,1)S(1)}, u32[]{:S(2)}, u32[]{:S(2)}) collective-permute-start(bf16[8,32,128]{2,1,0:T(8,128)(2,1)} %get-tuple-element.26), channel_id=1, source_target_pairs={{0,8},{8,0},{16,24},{24,16},{1,9},{9,1},{17,25},{25,17},{2,10},{10... | collective-permute-start | bytes 196616 | tf_op jit(solution)/shard_map/ppermute | solution.py:280
  8.9 4.5 %collective-permute-start.1 = (bf16[8,32,128]{2,1,0:T(8,128)(2,1)}, bf16[8,32,128]{2,1,0:T(8,128)(2,1)S(1)}, u32[]{:S(2)}, u32[]{:S(2)}) collective-permute-start(bf16[8,32,128]{2,1,0:T(8,128)(2,1)} %get-tuple-element.27), channel_id=1, source_target_pairs={{0,16},{8,24},{16,0},{24,8},{1,17},{9,25},{17,1},{25,9},{2,18},{10... | collective-permute-start | bytes 196616 | tf_op jit(solution)/shard_map/ppermute | solution.py:280
  10.4 5.4 %collective-permute-start.2 = (bf16[8,32,128]{2,1,0:T(8,128)(2,1)}, bf16[8,32,128]{2,1,0:T(8,128)(2,1)S(1)}, u32[]{:S(2)}, u32[]{:S(2)}) collective-permute-start(bf16[8,32,128]{2,1,0:T(8,128)(2,1)} %get-tuple-element.28), channel_id=1, source_target_pairs={{0,24},{8,16},{16,8},{24,0},{1,25},{9,17},{17,9},{25,1},{2,26},{10... | collective-permute-start | bytes 196616 | tf_op jit(solution)/shard_map/ppermute | solution.py:280
  11.6 4.2 %copy-start = (bf16[8,32,128]{2,1,0:T(8,128)(2,1)}, bf16[8,32,128]{2,1,0:T(8,128)(2,1)S(1)}, u32[]{:S(2)}) copy-start(bf16[8,32,128]{2,1,0:T(8,128)(2,1)S(1)} %collective-permute-done.refs_1_) | copy-start | bytes 196612
  28.2 16.5 %collective-permute-start.7 = (f32[4,2,150,128]{3,0,2,1:T(4,128)S(1)}, f32[4,2,150,128]{3,0,2,1:T(4,128)S(1)}, u32[]{:S(2)}, u32[]{:S(2)}) collective-permute-start(f32[4,2,150,128]{3,0,2,1:T(4,128)S(1)} %copy.11), channel_id=1, source_target_pairs={{0,1},{1,0},{2,3},{3,2},{4,5},{5,4},{6,7},{7,6},{8,9},{9,8},{10,11... | collective-permute-start | bytes 1843208 | tf_op jit(solution)/shard_map/ppermute | solution.py:289
  44.1 7.0 %collective-permute-start.3 = (f32[4,2,150,128]{3,0,2,1:T(4,128)S(1)}, f32[4,2,150,128]{3,0,2,1:T(4,128)S(1)}, u32[]{:S(2)}, u32[]{:S(2)}) collective-permute-start(f32[4,2,150,128]{3,0,2,1:T(4,128)S(1)} %copy.9), channel_id=1, source_target_pairs={{0,1},{1,0},{2,3},{3,2},{4,5},{5,4},{6,7},{7,6},{8,9},{9,8},{10,11... | collective-permute-start | bytes 1843208 | tf_op jit(solution)/shard_map/ppermute | solution.py:289
  47.6 7.2 %collective-permute-start.8 = (bf16[2,150,128]{2,1,0:T(8,128)(2,1)}, bf16[2,150,128]{2,1,0:T(8,128)(2,1)S(1)}, u32[]{:S(2)}, u32[]{:S(2)}) collective-permute-start(bf16[2,150,128]{2,1,0:T(8,128)(2,1)} %get-tuple-element.38), channel_id=1, source_target_pairs={{0,8},{8,0},{16,24},{24,16},{1,9},{9,1},{17,25},{25,17},{2,10},{10... | collective-permute-start | bytes 230408 | tf_op jit(solution)/shard_map/ppermute | solution.py:280
  48.2 9.4 %collective-permute-start.9 = (bf16[2,150,128]{2,1,0:T(8,128)(2,1)}, bf16[2,150,128]{2,1,0:T(8,128)(2,1)S(1)}, u32[]{:S(2)}, u32[]{:S(2)}) collective-permute-start(bf16[2,150,128]{2,1,0:T(8,128)(2,1)} %get-tuple-element.39), channel_id=1, source_target_pairs={{0,16},{8,24},{16,0},{24,8},{1,17},{9,25},{17,1},{25,9},{2,18},{10... | collective-permute-start | bytes 230408 | tf_op jit(solution)/shard_map/ppermute | solution.py:280
  48.5 9.1 %collective-permute-start.10 = (bf16[2,150,128]{2,1,0:T(8,128)(2,1)}, bf16[2,150,128]{2,1,0:T(8,128)(2,1)S(1)}, u32[]{:S(2)}, u32[]{:S(2)}) collective-permute-start(bf16[2,150,128]{2,1,0:T(8,128)(2,1)} %get-tuple-element.40), channel_id=1, source_target_pairs={{0,24},{8,16},{16,8},{24,0},{1,25},{9,17},{17,9},{25,1},{2,26},{10... | collective-permute-start | bytes 230408 | tf_op jit(solution)/shard_map/ppermute | solution.py:280
  54.0 5.1 %collective-permute-start.4 = (bf16[2,150,128]{2,1,0:T(8,128)(2,1)}, bf16[2,150,128]{2,1,0:T(8,128)(2,1)S(1)}, u32[]{:S(2)}, u32[]{:S(2)}) collective-permute-start(bf16[2,150,128]{2,1,0:T(8,128)(2,1)} %get-tuple-element.32), channel_id=1, source_target_pairs={{0,8},{8,0},{16,24},{24,16},{1,9},{9,1},{17,25},{25,17},{2,10},{10... | collective-permute-start | bytes 230408 | tf_op jit(solution)/shard_map/ppermute | solution.py:280
  54.6 4.6 %collective-permute-start.5 = (bf16[2,150,128]{2,1,0:T(8,128)(2,1)}, bf16[2,150,128]{2,1,0:T(8,128)(2,1)S(1)}, u32[]{:S(2)}, u32[]{:S(2)}) collective-permute-start(bf16[2,150,128]{2,1,0:T(8,128)(2,1)} %get-tuple-element.33), channel_id=1, source_target_pairs={{0,16},{8,24},{16,0},{24,8},{1,17},{9,25},{17,1},{25,9},{2,18},{10... | collective-permute-start | bytes 230408 | tf_op jit(solution)/shard_map/ppermute | solution.py:280
  54.9 5.5 %copy-start.3 = (bf16[2,150,128]{2,1,0:T(8,128)(2,1)}, bf16[2,150,128]{2,1,0:T(8,128)(2,1)S(1)}, u32[]{:S(2)}) copy-start(bf16[2,150,128]{2,1,0:T(8,128)(2,1)S(1)} %collective-permute-done.8.rest_5_) | copy-start | bytes 230404
  54.9 5.5 %collective-permute-start.6 = (bf16[2,150,128]{2,1,0:T(8,128)(2,1)}, bf16[2,150,128]{2,1,0:T(8,128)(2,1)S(1)}, u32[]{:S(2)}, u32[]{:S(2)}) collective-permute-start(bf16[2,150,128]{2,1,0:T(8,128)(2,1)} %get-tuple-element.34), channel_id=1, source_target_pairs={{0,24},{8,16},{16,8},{24,0},{1,25},{9,17},{17,9},{25,1},{2,26},{10... | collective-permute-start | bytes 230408 | tf_op jit(solution)/shard_map/ppermute | solution.py:280
  66.2 4.8 %collective-permute-start.11 = (bf16[304,128]{1,0:T(8,128)(2,1)}, bf16[304,128]{1,0:T(8,128)(2,1)S(1)}, u32[]{:S(2)}, u32[]{:S(2)}) collective-permute-start(bf16[304,128]{1,0:T(8,128)(2,1)} %get-tuple-element.42), channel_id=1, source_target_pairs={{0,2},{1,3},{2,0},{3,1},{4,6},{5,7},{6,4},{7,5},{8,10},{9,11},{10,... | collective-permute-start | bytes 233480 | tf_op jit(solution)/shard_map/ppermute | solution.py:286
  67.9 7.1 %collective-permute-start.12 = (bf16[304,128]{1,0:T(8,128)(2,1)}, bf16[304,128]{1,0:T(8,128)(2,1)S(1)}, u32[]{:S(2)}, u32[]{:S(2)}) collective-permute-start(bf16[304,128]{1,0:T(8,128)(2,1)} %get-tuple-element.43), channel_id=1, source_target_pairs={{0,4},{1,5},{2,6},{3,7},{4,0},{5,1},{6,2},{7,3},{8,12},{9,13},{10,... | collective-permute-start | bytes 233480 | tf_op jit(solution)/shard_map/ppermute | solution.py:286
  70.5 6.4 %collective-permute-start.13 = (bf16[304,128]{1,0:T(8,128)(2,1)}, bf16[304,128]{1,0:T(8,128)(2,1)S(1)}, u32[]{:S(2)}, u32[]{:S(2)}) collective-permute-start(bf16[304,128]{1,0:T(8,128)(2,1)} %get-tuple-element.44), channel_id=1, source_target_pairs={{0,6},{1,7},{2,4},{3,5},{4,2},{5,3},{6,0},{7,1},{8,14},{9,15},{10,... | collective-permute-start | bytes 233480 | tf_op jit(solution)/shard_map/ppermute | solution.py:286
  71.0 5.9 %copy-start.16 = (bf16[304,128]{1,0:T(8,128)(2,1)}, bf16[304,128]{1,0:T(8,128)(2,1)S(1)}, u32[]{:S(2)}) copy-start(bf16[304,128]{1,0:T(8,128)(2,1)S(1)} %collective-permute-done.11.refs_1_) | copy-start | bytes 233476
  79.3 6.5 %collective-permute-start.16 = (bf16[304,128]{1,0:T(8,128)(2,1)}, bf16[304,128]{1,0:T(8,128)(2,1)S(1)}, u32[]{:S(2)}, u32[]{:S(2)}) collective-permute-start(bf16[304,128]{1,0:T(8,128)(2,1)} %shard_map.61.refs_0_), channel_id=1, source_target_pairs={{0,6},{1,7},{2,4},{3,5},{4,2},{5,3},{6,0},{7,1},{8,14},{9,15},{10,... | collective-permute-start | bytes 233480 | tf_op jit(solution)/shard_map/ppermute | solution.py:286
  80.2 7.1 %collective-permute-start.15 = (bf16[304,128]{1,0:T(8,128)(2,1)}, bf16[304,128]{1,0:T(8,128)(2,1)S(1)}, u32[]{:S(2)}, u32[]{:S(2)}) collective-permute-start(bf16[304,128]{1,0:T(8,128)(2,1)} %shard_map.61.refs_0_), channel_id=1, source_target_pairs={{0,4},{1,5},{2,6},{3,7},{4,0},{5,1},{6,2},{7,3},{8,12},{9,13},{10,... | collective-permute-start | bytes 233480 | tf_op jit(solution)/shard_map/ppermute | solution.py:286
  80.3 7.1 %collective-permute-start.14 = (bf16[304,128]{1,0:T(8,128)(2,1)}, bf16[304,128]{1,0:T(8,128)(2,1)S(1)}, u32[]{:S(2)}, u32[]{:S(2)}) collective-permute-start(bf16[304,128]{1,0:T(8,128)(2,1)} %shard_map.61.refs_0_), channel_id=1, source_target_pairs={{0,2},{1,3},{2,0},{3,1},{4,6},{5,7},{6,4},{7,5},{8,10},{9,11},{10,... | collective-permute-start | bytes 233480 | tf_op jit(solution)/shard_map/ppermute | solution.py:286
  83.6 4.2 %collective-permute-start.17 = (bf16[304,128]{1,0:T(8,128)(2,1)}, bf16[304,128]{1,0:T(8,128)(2,1)S(1)}, u32[]{:S(2)}, u32[]{:S(2)}) collective-permute-start(bf16[304,128]{1,0:T(8,128)(2,1)} %shard_map.61.refs_0_), channel_id=1, source_target_pairs={{0,1},{1,0},{2,3},{3,2},{4,5},{5,4},{6,7},{7,6},{8,9},{9,8},{10,11... | collective-permute-start | bytes 233480 | tf_op jit(solution)/shard_map/ppermute | solution.py:289
  85.8 2.1 %collective-permute-start.20 = (bf16[304,128]{1,0:T(8,128)(2,1)S(1)}, bf16[304,128]{1,0:T(8,128)(2,1)S(1)}, u32[]{:S(2)}, u32[]{:S(2)}) collective-permute-start(bf16[304,128]{1,0:T(8,128)(2,1)S(1)} %collective-permute-done.16.refs_3_), channel_id=1, source_target_pairs={{0,1},{1,0},{2,3},{3,2},{4,5},{5,4},{6,7},{7,6},{8,9},{9,8},{10,11... | collective-permute-start | bytes 233480 | tf_op jit(solution)/shard_map/ppermute | solution.py:289
  87.3 1.3 %collective-permute-start.19 = (bf16[304,128]{1,0:T(8,128)(2,1)S(1)}, bf16[304,128]{1,0:T(8,128)(2,1)S(1)}, u32[]{:S(2)}, u32[]{:S(2)}) collective-permute-start(bf16[304,128]{1,0:T(8,128)(2,1)S(1)} %collective-permute-done.15.refs_2_), channel_id=1, source_target_pairs={{0,1},{1,0},{2,3},{3,2},{4,5},{5,4},{6,7},{7,6},{8,9},{9,8},{10,11... | collective-permute-start | bytes 233480 | tf_op jit(solution)/shard_map/ppermute | solution.py:289
  87.4 1.4 %collective-permute-start.18 = (bf16[304,128]{1,0:T(8,128)(2,1)S(1)}, bf16[304,128]{1,0:T(8,128)(2,1)S(1)}, u32[]{:S(2)}, u32[]{:S(2)}) collective-permute-start(bf16[304,128]{1,0:T(8,128)(2,1)S(1)} %collective-permute-done.14.refs_1_), channel_id=1, source_target_pairs={{0,1},{1,0},{2,3},{3,2},{4,5},{5,4},{6,7},{7,6},{8,9},{9,8},{10,11... | collective-permute-start | bytes 233480 | tf_op jit(solution)/shard_map/ppermute | solution.py:289
  (16 other events, 23.4 us)
where the time goes:
time: 96.2 us; the launch traced here: 95.6 us
  Pallas kernels  42.7 us (44%)
  starting transfers between devices  21.4 us (22%)
  waiting for transfers between devices  19.2 us (20%)
  local copies, waits for them, and re-layouts  12.3 us (13%)
    pallas_call x8, Pallas kernels, call(): pl.pallas_call(body, out_shape=out_shapes, in_specs=in_specs or [whole] *...  42.7 us
    ppermute x9, starting transfers between devices, over_freq(): lax.ppermute(values[k], 'freq', [(i, i ^ k) for i in range(freq)])  11.5 us
    ppermute x6, waiting for transfers between devices, to_piece(): return lax.ppermute(value, 'param', pairs)  10.1 us
    ppermute x6, starting transfers between devices, to_piece(): return lax.ppermute(value, 'param', pairs)  8.77 us
    ppermute x9, waiting for transfers between devices, over_freq(): lax.ppermute(values[k], 'freq', [(i, i ^ k) for i in range(freq)])  8.2 us
    pallas_call x3, local copies, waits for them, and re-layouts, call(): pl.pallas_call(body, out_shape=out_shapes, in_specs=in_specs or [whole] *...  5.37 us
    unnamed x39, local copies, waits for them, and re-layouts  5.11 us
  transfers between devices with their start and end apart: 21, of which 13 were waited for; matrix products, arithmetic and copies ran while one was open for 3% of the time, Pallas kernels for 19%

commit v1 on v0

v1 whole, which is shorter than its diff:
```python
import functools
import math

import jax
import jax.numpy as jnp
import numpy as np
from jax import lax
from jax.experimental import pallas as pl
from jax.experimental.pallas import tpu as pltpu
from jax.sharding import PartitionSpec as P

LANES = 128
BF16, F32, I32 = jnp.bfloat16, jnp.float32, jnp.int32
VMEM = pltpu.VMEM
MIB = 1024 * 1024
LIMIT = 16 * MIB
FULL = 67043328
ROOM = 10 * MIB + 400 * 1024
CHUNK, EARLY, AHEAD = 8, 5, 3


def up(value, unit):
    return -(-value // unit) * unit


def dot_nt(left, right):
    return lax.dot_general(left, right, (((1,), (1,)), ((), ())), preferred_element_type=F32)


def dot_nn(left, right):
    return jnp.dot(left, right, preferred_element_type=F32)


def halves(value):
    high = value.astype(BF16)
    return high, (value - high.astype(F32)).astype(BF16)


class Plan:
    def __init__(self, mesh, sources, kernel, bin_of_slot):
        self.freq = mesh.shape["freq"]
        self.param = mesh.shape["param"]
        self.pieces = self.param // 2
        self.count, self.steps, self.mine = sources.shape
        self.slots = bin_of_slot.shape[0]
        self.here, _, self.sensors, self.depth = kernel.shape
        self.half = self.count // 2
        self.comps = 2 * self.half
        self.group = LANES // self.comps
        self.groups = -(-self.here // self.group)
        self.block = self.sensors // self.freq
        self.block_pad = up(self.block, 8)
        self.bins = up(self.steps + 1, LANES)
        self.span = -(-self.steps // self.pieces)
        self.span_pad = up(self.span, LANES)
        self.slots_pad = up(self.slots, LANES)
        self.last = self.here - (self.groups - 1) * self.group
        self.fold = self.group // self.last
        self.fold_rows = up(-(-self.block_pad // self.fold), 8)
        self.share_rows = (self.groups - 1) * self.block_pad + self.fold_rows
        self.rows = self.half * self.block_pad
        self.spare = self.span_pad - self.span
        self.base = self.rows
        if self.spare:
            self.cuts = -(-self.span // self.spare)
            while (self.rows - self.base + 16) * self.cuts <= self.base - 16:
                self.base -= 16
        self.tail = self.rows - self.base
        assert self.here <= LANES and self.depth == self.mine * self.freq
        assert self.freq & (self.freq - 1) == 0 and self.pieces & (self.pieces - 1) == 0

    def tables(self):
        times = np.arange(self.steps)
        rows = times // self.span * self.span_pad + times % self.span
        bins = np.arange(self.steps + 1)
        angle = (times[:, None] * bins[None, :] % (2 * self.steps)) * (math.pi / self.steps)
        table = np.zeros((self.pieces * self.span_pad, 2 * self.bins), np.float64)
        table[rows, : self.steps + 1] = np.cos(angle)
        table[rows, self.bins : self.bins + self.steps + 1] = np.sin(angle)
        high = table.astype(jnp.bfloat16)
        low = (table - high.astype(np.float64)).astype(jnp.bfloat16)
        return high, low


def pack(plan, value):
    if not plan.tail:
        return value
    tail, parts = value[plan.base :], []
    for j in range(plan.cuts):
        parts.append(pltpu.roll(tail, (plan.span - plan.spare * j) % plan.span_pad, 1))
    left = plan.base - plan.tail * plan.cuts
    if left:
        parts.append(jnp.zeros((left, plan.span_pad), F32))
    lane = lax.broadcasted_iota(I32, (plan.base, plan.span_pad), 1)
    return jnp.where(lane < plan.span, value[: plan.base], jnp.concatenate(parts, axis=0))


def unpack(plan, value):
    if not plan.tail:
        return value
    tail = jnp.zeros((plan.tail, plan.span_pad), F32)
    lane = lax.broadcasted_iota(I32, tail.shape, 1)
    for j in range(plan.cuts):
        part = value[plan.tail * j : plan.tail * (j + 1)]
        part = pltpu.roll(part, (plan.spare * j - plan.span) % plan.span_pad, 1)
        tail = jnp.where(lane // plan.spare == j, part, tail)
    return jnp.concatenate([value, tail], axis=0)


def bin_row(plan, bins_ref, row_ref):
    row_ref[...] = jnp.full(row_ref.shape, -1, I32)
    row_ref[0:1, 0 : plan.slots] = bins_ref[...]
    return row_ref[0:1, :]


def slot_hits(plan, row, shard):
    shift = (-plan.here * shard) % plan.slots_pad
    if shift:
        row = pltpu.roll(row, shift, 1)
    row = row[:, :LANES]
    lane = lax.broadcasted_iota(I32, (1, LANES), 1)
    row = jnp.where(lane < plan.here, row, -1)
    bins = lax.broadcasted_iota(I32, (plan.bins, LANES), 0)
    return jnp.where(bins == row, 1.0, 0.0).astype(BF16)


def stream(kern_ref, first, size, target, sem_ref, index):
    return pltpu.make_async_copy(
        kern_ref.at[pl.ds(first, size)], target.at[pl.ds(0, size)], sem_ref.at[index]
    )


def forward_kernel(plan, *refs):
    ins, outs, rest = refs[:4], refs[4 : 4 + plan.freq], refs[4 + plan.freq :]
    bins_ref, src_ref, high_ref, low_ref, row_ref, time_ref, send_ref, sem_ref = rest
    copies = [
        pltpu.make_async_copy(source, target, sem_ref.at[i])
        for i, (source, target) in enumerate(zip(ins, rest))
    ]
    for copy in copies:
        copy.start()
    for copy in copies:
        copy.wait()
    me = lax.axis_index("freq")
    time_ref[...] = jnp.zeros(time_ref.shape, F32)
    rows = plan.count * plan.mine
    for z in range(plan.pieces):
        first = z * plan.span
        size = min(plan.span, plan.steps - first)
        at = z * plan.span_pad
        time_ref[:, at : at + size] = src_ref[:, :, first : first + size].reshape(rows, size)
    high, low = halves(time_ref[...])
    spectrum = (
        dot_nn(high, high_ref[...]) + dot_nn(high, low_ref[...]) + dot_nn(low, high_ref[...])
    )
    scale = 1.0 / math.sqrt(plan.steps)
    both = jnp.concatenate(
        [
            (spectrum[:, : plan.bins] * scale).astype(BF16),
            (spectrum[:, plan.bins :] * -scale).astype(BF16),
        ],
        axis=0,
    )
    row = bin_row(plan, bins_ref, row_ref)
    for shard in range(plan.freq):
        picked = dot_nn(both, slot_hits(plan, row, shard))
        for c in range(plan.count):
            for part in range(2):
                first = part * rows + c * plan.mine
                comp = 2 * (c % plan.half) + part
                value = picked[first : first + plan.mine]
                if comp:
                    value = pltpu.roll(value, comp * plan.group, 1)
                send_ref[shard, 2 * c + part] = value.astype(BF16)
    for k in range(plan.freq):
        outs[k][...] = send_ref[me ^ k]


def load_kernel(plan, count, after_ref, bins_ref, kern_ref, out_ref, hits_ref, row_ref, sem_ref):
    starts = range(0, count, CHUNK)
    copies = [
        stream(kern_ref, at, min(CHUNK, count - at), out_ref.at[pl.ds(at, CHUNK)], sem_ref, i)
        for i, at in enumerate(starts)
    ]
    for copy in copies:
        copy.start()
    row = bin_row(plan, bins_ref, row_ref)
    for shard in range(plan.freq):
        hits_ref[shard] = slot_hits(plan, row, shard)
    for copy in copies:
        copy.wait()


def response_kernel(plan, begin, end, held, ahead, *refs):
    freq, group = plan.freq, plan.group
    arrived, refs = refs[:freq], refs[freq:]
    held_refs, kern_ref, refs = refs[: len(held)], refs[len(held)], refs[len(held) + 1 :]
    places = [(ref, at) for ref, size in zip(held_refs, held) for at in range(size)]
    ready = len(places)
    own_ref, other_ref, refs = refs[0], refs[1], refs[2:]
    if ahead:
        ahead_ref, refs = refs[0], refs[1:]
    buf_ref, spec_ref, rhs_ref, sem_ref = refs
    first_group, last_group = begin, end
    first = first_group * group
    total = min(last_group * group, plan.here) - first
    copies, late = {}, []
    for at in range(ready, total, CHUNK):
        size = min(CHUNK, total - at)
        target = buf_ref.at[pl.ds(at - ready, size)]
        copies[at] = stream(kern_ref, first + at, size, target, sem_ref, len(copies))
    for at in range(0, ahead, CHUNK):
        size = min(CHUNK, ahead - at)
        target = ahead_ref.at[pl.ds(at, size)]
        index = len(copies) + len(late)
        late.append(stream(kern_ref, first + total + at, size, target, sem_ref, index))
    for copy in [*copies.values(), *late]:
        copy.start()
    me, core = lax.axis_index("freq"), lax.axis_index("param") % 2
    for k in range(freq):
        at = pl.multiple_of((me ^ k) * plan.mine, plan.mine)
        spec_ref[:, pl.ds(at, plan.mine), :] = arrived[k][...]
    lane = lax.broadcasted_iota(I32, (plan.depth, LANES), 1)
    for g in range(first_group, last_group):
        for side in range(2):
            base = (core ^ side) * plan.comps
            place = (lane // group - g) % plan.comps
            real = spec_ref[base].astype(F32)
            for comp in range(1, plan.comps):
                real = jnp.where(place == comp, spec_ref[base + comp].astype(F32), real)
            imag = jnp.where(
                place % 2 == 0, -pltpu.roll(real, LANES - group, 1), pltpu.roll(real, group, 1)
            )
            cols = slice(side * LANES, (side + 1) * LANES)
            rhs_ref[g - first_group, : plan.depth, cols] = real.astype(BF16)
            rhs_ref[g - first_group, plan.depth :, cols] = imag.astype(BF16)
    within = lax.broadcasted_iota(I32, (2 * plan.depth, 2 * LANES), 1) % group

    def multiply(acc_even, acc_odd):
        accs = (acc_even, acc_odd)

        def push(slot):
            weights = rhs_ref[slot // group]
            pltpu.matmul_push_rhs(
                jnp.where(within == slot % group, weights, jnp.zeros_like(weights)),
                staging_register=slot // 2 % 2,
                mxu_index=slot % 2,
            )

        for acc in accs:
            pltpu.matmul_pop(acc)
        for slot in range(min(2, total)):
            push(slot)
        for slot in range(total):
            if slot + 2 < total:
                push(slot + 2)
            if slot in copies:
                copies[slot].wait()
            ref, at = places[slot] if slot < ready else (buf_ref, slot - ready)
            both = [ref[at, part] for part in range(2)]
            left = jnp.concatenate(both, axis=1)
            if left.shape[0] % 16:
                left = jnp.concatenate([left, left[:8]], axis=0)
            pltpu.matmul_acc_lhs(accs[slot % 2], left, load_staged_rhs=slot // 2 % 2)
            if (slot + 1) % group == 0 or slot + 1 == total:
                g = slot // group
                value = pltpu.matmul_pop(acc_even) + pltpu.matmul_pop(acc_odd)
                for f in range(freq):
                    rows = value[f * plan.block : (f + 1) * plan.block]
                    at = (f * (last_group - first_group) + g) * plan.block_pad
                    own_ref[at : at + plan.block] = rows[:, :LANES]
                    other_ref[at : at + plan.block] = rows[:, LANES:]

    shape = (up(plan.sensors, 16), 2 * LANES)
    pl.run_scoped(multiply, pltpu.ACC(0)(shape, F32), pltpu.ACC(1)(shape, F32))
    for copy in late:
        copy.wait()


def join_kernel(plan, sizes, *refs):
    pairs, outs = refs[: 2 * len(sizes)], refs[2 * len(sizes) :]
    me, pad, fold_rows = lax.axis_index("freq"), plan.block_pad, plan.fold_rows
    lane = lax.broadcasted_iota(I32, (fold_rows, LANES), 1) % plan.group
    for k in range(plan.freq):
        done = 0
        for call_at, size in enumerate(sizes):
            own_ref, other_ref = pairs[2 * call_at : 2 * call_at + 2]
            at = pl.multiple_of((me ^ k) * (size * pad), 8)
            value = own_ref[pl.ds(at, size * pad)] + other_ref[pl.ds(at, size * pad)]
            full = min(size, plan.groups - 1 - done) * pad
            if full:
                outs[k][done * pad : done * pad + full] = value[:full].astype(BF16)
            done += size
        tile, packed = value[full:], jnp.zeros((fold_rows, LANES), F32)
        for j in range(plan.fold):
            part = tile[j * fold_rows : (j + 1) * fold_rows]
            if part.shape[0] < fold_rows:
                rest = jnp.zeros((fold_rows - part.shape[0], LANES), F32)
                part = jnp.concatenate([part, rest], axis=0)
            if j:
                part = pltpu.roll(part, j * plan.last, 1)
            packed = jnp.where(lane // plan.last == j, part, packed)
        outs[k][plan.share_rows - fold_rows :] = packed.astype(BF16)


def inverse_kernel(plan, hits_ref, high_ref, low_ref, *rest):
    freq, group, pad = plan.freq, plan.group, plan.block_pad
    arrived, rest = rest[:freq], rest[freq:]
    outs, (joined_ref,) = rest[: plan.pieces], rest[plan.pieces :]
    me, piece = lax.axis_index("freq"), lax.axis_index("param") // 2
    lane = lax.broadcasted_iota(I32, (pad, LANES), 1)
    real_row = lax.broadcasted_iota(I32, (pad, LANES), 0) < plan.block
    for k in range(freq):
        starts = range(0, (plan.groups - 1) * pad, pad)
        tiles = [arrived[k][at : at + pad].astype(F32) for at in starts]
        packed = arrived[k][plan.share_rows - plan.fold_rows :].astype(F32)
        folds = [packed] + [
            pltpu.roll(packed, LANES - j * plan.last, 1) for j in range(1, plan.fold)
        ]
        tiles.append(jnp.concatenate(folds, axis=0)[:pad])
        for comp in range(plan.comps):
            value = jnp.zeros((pad, LANES), F32)
            for g, tile in enumerate(tiles):
                inside = (lane // group == (g + comp) % plan.comps) & real_row
                value = jnp.where(inside, tile, value)
            if comp:
                value = pltpu.roll(value, LANES - comp * group, 1)
            at = comp * pad
            joined_ref[at : at + pad, k * LANES : (k + 1) * LANES] = value.astype(BF16)
    hits = jnp.concatenate([hits_ref[me ^ k] for k in range(freq)], axis=1)
    by_bin = dot_nt(joined_ref[...], hits)
    bins = lax.broadcasted_iota(I32, (1, plan.bins), 1)
    weight = jnp.where((bins == 0) | (bins == plan.steps), 1.0, 2.0)
    rows = []
    for c in range(plan.half):
        real = by_bin[2 * c * pad : (2 * c + 1) * pad] * weight
        imag = by_bin[(2 * c + 1) * pad : (2 * c + 2) * pad] * -weight
        rows.append(jnp.concatenate([real, imag], axis=1).astype(BF16))
    high = jnp.concatenate(rows, axis=0)
    scale = 1.0 / math.sqrt(2.0 * (plan.steps + 1))
    for k in range(plan.pieces):
        at = pl.multiple_of((piece ^ k) * plan.span_pad, plan.span_pad)
        table_high = high_ref[pl.ds(at, plan.span_pad), :]
        table_low = low_ref[pl.ds(at, plan.span_pad), :]
        value = (dot_nt(high, table_high) + dot_nt(high, table_low)) * scale
        outs[k][...] = pack(plan, value).astype(outs[k].dtype)


def stack_kernel(*refs):
    size = refs[0].shape[0]
    for k, ref in enumerate(refs[:-1]):
        refs[-1][k * size : (k + 1) * size] = ref[...]


def sum_kernel(*refs):
    value = refs[0][...]
    for ref in refs[1:-1]:
        value = value + ref[...].astype(F32)
    refs[-1][...] = value.astype(BF16)


def output_kernel(plan, *refs):
    out_ref = refs[-1]
    piece, core = lax.axis_index("param") // 2, lax.axis_index("param") % 2
    width = plan.span_pad
    time = lax.broadcasted_iota(I32, (plan.steps, plan.pieces * width), 0)
    lane = lax.broadcasted_iota(I32, (plan.steps, plan.pieces * width), 1)
    inside = lane % width
    target = (lane // width ^ piece) * plan.span + inside
    pick = jnp.where((time == target) & (inside < plan.span), 1.0, 0.0).astype(BF16)
    for side in range(2):
        parts = [
            unpack(plan, refs[side][k * plan.base : (k + 1) * plan.base].astype(F32)).astype(BF16)
            for k in range(plan.pieces)
        ]
        value = dot_nt(jnp.concatenate(parts, axis=1), pick)
        for c in range(plan.half):
            at = c * plan.block_pad
            out_ref[:, (core ^ side) * plan.half + c, :] = value[at : at + plan.block]


def cost(flops, moved):
    return pl.CostEstimate(flops=flops, bytes_accessed=moved, transcendentals=0)


def call(body, out_shapes, args, in_specs=None, scratch=(), cost=None, limit=LIMIT):
    whole = pl.BlockSpec(memory_space=VMEM)
    return pl.pallas_call(
        body,
        out_shape=out_shapes,
        in_specs=in_specs or [whole] * len(args),
        out_specs=jax.tree.map(lambda _: whole, out_shapes),
        scratch_shapes=list(scratch),
        cost_estimate=cost,
        compiler_params=pltpu.CompilerParams(vmem_limit_bytes=limit),
    )(*args)


def shards(mesh, sources, kernel, bin_of_slot):
    plan = Plan(mesh, sources, kernel, bin_of_slot)
    freq, pieces = plan.freq, plan.pieces
    shape = jax.ShapeDtypeStruct
    high, low = plan.tables()
    bins = bin_of_slot.reshape(1, plan.slots)
    row = VMEM((8, plan.slots_pad), I32)
    whole = pl.BlockSpec(memory_space=VMEM)

    def over_freq(values):
        return [values[0]] + [
            lax.ppermute(values[k], "freq", [(i, i ^ k) for i in range(freq)])
            for k in range(1, freq)
        ]

    def to_piece(value, k):
        pairs = [(2 * z + h, 2 * (z ^ k) + h) for z in range(pieces) for h in range(2)]
        return lax.ppermute(value, "param", pairs)

    def to_core(value):
        return lax.ppermute(value, "param", [(i, i ^ 1) for i in range(plan.param)])

    middle = -(-plan.groups // 2)
    ranges = [(0, middle), (middle, plan.groups)]
    sizes = [end - begin for begin, end in ranges]
    totals = [min(end * plan.group, plan.here) - begin * plan.group for begin, end in ranges]
    block = (2, plan.sensors, plan.depth)
    early = min(totals[0] // CHUNK, EARLY) * CHUNK

    spectra = call(
        functools.partial(forward_kernel, plan),
        [shape((2 * plan.count, plan.mine, LANES), BF16)] * freq,
        (bins, jnp.transpose(sources, (0, 2, 1)), high, low),
        in_specs=[pl.BlockSpec(memory_space=pltpu.HBM)] * 4,
        scratch=[
            VMEM(bins.shape, I32),
            VMEM((plan.count, plan.mine, plan.steps), F32),
            VMEM(high.shape, BF16),
            VMEM(low.shape, BF16),
            row,
            VMEM((plan.count * plan.mine, pieces * plan.span_pad), F32),
            VMEM((freq, 2 * plan.count, plan.mine, LANES), BF16),
            pltpu.SemaphoreType.DMA((4,)),
        ],
        cost=cost(2 * 10**9, 2 * high.size),
        limit=FULL - ROOM,
    )
    arrived = over_freq(spectra)

    hbm = pl.BlockSpec(memory_space=pltpu.HBM)
    ready, hits = call(
        functools.partial(load_kernel, plan, early),
        [shape((early, *block), BF16), shape((freq, plan.bins, LANES), BF16)],
        (spectra[0], bins, kernel),
        in_specs=[pl.BlockSpec(memory_space=pl.ANY), whole, hbm],
        scratch=[row, pltpu.SemaphoreType.DMA((-(-early // CHUNK),))],
        cost=cost(4 * 10**9, 4 * early * plan.sensors * plan.depth),
    )
    ready = [ready]
    pairs = []
    for index, (begin, end) in enumerate(ranges):
        total, held = totals[index], [array.shape[0] for array in ready]
        rest = total - sum(held)
        ahead = 0 if index else min(totals[1] // CHUNK, AHEAD) * CHUNK
        size = shape((freq * sizes[index] * plan.block_pad, LANES), F32)
        own, other, *later = call(
            functools.partial(response_kernel, plan, begin, end, held, ahead),
            [size, size] + ([shape((ahead, *block), BF16)] if ahead else []),
            (*arrived, *ready, kernel),
            in_specs=[whole] * (freq + len(ready)) + [hbm],
            scratch=[
                VMEM((max(rest, CHUNK), *block), BF16),
                VMEM((2 * plan.count, plan.depth, LANES), BF16),
                VMEM((end - begin, 2 * plan.depth, 2 * LANES), BF16),
                pltpu.SemaphoreType.DMA((-(-rest // CHUNK) + ahead // CHUNK + 1,)),
            ],
            cost=cost(total * 512 * plan.sensors * plan.depth, 4 * total * plan.sensors * plan.depth),
        )
        ready = later
        pairs += [own, to_core(other)]
    joined = call(
        functools.partial(join_kernel, plan, sizes),
        [shape((plan.share_rows, LANES), BF16)] * freq,
        pairs,
    )
    parts = over_freq(joined)

    partial = call(
        functools.partial(inverse_kernel, plan),
        [shape((plan.base, plan.span_pad), BF16 if k else F32) for k in range(pieces)],
        (hits, high, low, *parts),
        scratch=[
            VMEM((plan.comps * plan.block_pad, freq * LANES), BF16),
        ],
    )
    received = [to_piece(partial[k], k) for k in range(1, pieces)]
    piece = call(sum_kernel, shape((plan.base, plan.span_pad), BF16), (partial[0], *received))
    mine = [piece] + [to_piece(piece, k) for k in range(1, pieces)]
    mine = call(stack_kernel, shape((pieces * plan.base, plan.span_pad), BF16), mine)
    theirs = to_core(mine)
    by_sensor = call(
        functools.partial(output_kernel, plan),
        shape((plan.block, plan.count, plan.steps), F32),
        (mine, theirs),
    )
    return jnp.transpose(by_sensor, (1, 2, 0))


def solution(mesh):
    return jax.shard_map(
        functools.partial(shards, mesh),
        mesh=mesh,
        in_specs=(P(None, None, ("param", "freq")), P("freq", None, None, "param"), P()),
        out_specs=P(None, None, "freq"),
        check_vma=False,
    )
```

time: 96.2 us -> 59.2 us (0.62)
  Pallas kernels: 42.7 us -> 21.6 us
  local copies, waits for them, and re-layouts: 12.3 us -> 0.69 us
  starting transfers between devices: 21.4 us -> 17.7 us
    pallas_call x8 -> x9, Pallas kernels: 42.7 us -> 21.6 us  [call(): pl.pallas_call(body, out_shape=out_shapes, in_specs=in_specs or [whole] *...]
    pallas_call x3 -> x0, local copies, waits for them, and re-layouts: 5.37 us -> none  [call(): pl.pallas_call(body, out_shape=out_shapes, in_specs=in_specs or [whole] *...]
    unnamed x39 -> x6, local copies, waits for them, and re-layouts: 5.11 us -> 0.69 us
    ppermute x9 -> x6, starting transfers between devices: 11.5 us -> 8.13 us  [over_freq(): lax.ppermute(values[k], 'freq', [(i, i ^ k) for i in range(freq)])]
    ppermute x6 -> x3, waiting for transfers between devices: 0.9 us -> 3.2 us  [to_core(): return lax.ppermute(value, 'param', [(i, i ^ 1) for i in range(plan.param)])]
    ppermute x2 -> x0, local copies, waits for them, and re-layouts: 1.77 us -> none  [to_core(): return lax.ppermute(value, 'param', [(i, i ^ 1) for i in range(plan.param)])]
    ppermute x9 -> x6, waiting for transfers between devices: 8.2 us -> 6.78 us  [over_freq(): lax.ppermute(values[k], 'freq', [(i, i ^ k) for i in range(freq)])]
    ppermute x6, waiting for transfers between devices: 10.1 us -> 9.03 us  [to_piece(): return lax.ppermute(value, 'param', pairs)]
  transfers between devices with their start and end apart: 21 -> 15, of which waited for: 13 -> 10; matrix products, arithmetic and copies ran while one was open for 3% -> 0% of each run, Pallas kernels for 19% -> 14%
where the time goes in v1:
time: 59.2 us; the launch traced here: 59.1 us
  Pallas kernels  21.6 us (36%)
  waiting for transfers between devices  19 us (32%)
  starting transfers between devices  17.7 us (30%)
  local copies, waits for them, and re-layouts  0.69 us (1%)
    pallas_call x9, Pallas kernels, call(): pl.pallas_call(body, out_shape=out_shapes, in_specs=in_specs or [whole] *...  21.6 us
    ppermute x6, waiting for transfers between devices, to_piece(): return lax.ppermute(value, 'param', pairs)  9.03 us
    ppermute x6, starting transfers between devices, to_piece(): return lax.ppermute(value, 'param', pairs)  8.9 us
    ppermute x6, starting transfers between devices, over_freq(): lax.ppermute(values[k], 'freq', [(i, i ^ k) for i in range(freq)])  8.13 us
    ppermute x6, waiting for transfers between devices, over_freq(): lax.ppermute(values[k], 'freq', [(i, i ^ k) for i in range(freq)])  6.78 us
    ppermute x3, waiting for transfers between devices, to_core(): return lax.ppermute(value, 'param', [(i, i ^ 1) for i in range(plan.param)])  3.2 us
  transfers between devices with their start and end apart: 15, of which 10 were waited for; matrix products, arithmetic and copies ran while one was open for 0% of the time, Pallas kernels for 14%

profile of v1, /device:TPU:0, one launch (start us, length us, event | category | flops | bytes accessed | tf_op | source)
XLA Modules:
  0.0 59.1 jit_solution(8315974102557389548)
XLA Ops:
  0.0 0.7 %copy-done.2 = s32[424]{0:T(512)S(1)} copy-done((s32[424]{0:T(512)S(1)}, s32[424]{0:T(512)}, u32[]{:S(2)}) %copy-start.2) | copy-done | bytes 1720
  0.7 2.8 %shard_map.55 = (bf16[8,32,128]{2,1,0:T(8,128)(2,1)S(1)}, bf16[8,32,128]{2,1,0:T(8,128)(2,1)S(1)}, bf16[8,32,128]{2,1,0:T(8,128)(2,1)S(1)}, bf16[8,32,128]{2,1,0:T(8,128)(2,1)S(1)}) custom-call(s32[1,424]{1,0:T(1,128)S(1)} %bitcast.3, f32[4,32,420]{2,1,0:T(8,128)} %bitcast.5, bf16[512,1024]{1,0:T(8,128)(2,1)} %constant.4.clone.refs_2_.high_ref, ...), custom_call_target="tpu_custom_call" | custom-call | flops 2000000000 | bytes 1048576 | tf_op jit(solution)/shard_map/pallas_call | solution.py:388
  3.5 3.0 %collective-permute-start = (bf16[8,32,128]{2,1,0:T(8,128)(2,1)S(1)}, bf16[8,32,128]{2,1,0:T(8,128)(2,1)S(1)}, u32[]{:S(2)}, u32[]{:S(2)}) collective-permute-start(bf16[8,32,128]{2,1,0:T(8,128)(2,1)S(1)} %get-tuple-element.26), channel_id=1, source_target_pairs={{0,8},{8,0},{16,24},{24,16},{1,9},{9,1},{17,25},{25,17},{2,10},{10... | collective-permute-start | bytes 196616 | tf_op jit(solution)/shard_map/ppermute | solution.py:410
  6.5 1.5 %collective-permute-start.1 = (bf16[8,32,128]{2,1,0:T(8,128)(2,1)S(1)}, bf16[8,32,128]{2,1,0:T(8,128)(2,1)S(1)}, u32[]{:S(2)}, u32[]{:S(2)}) collective-permute-start(bf16[8,32,128]{2,1,0:T(8,128)(2,1)S(1)} %get-tuple-element.27), channel_id=1, source_target_pairs={{0,16},{8,24},{16,0},{24,8},{1,17},{9,25},{17,1},{25,9},{2,18},{10... | collective-permute-start | bytes 196616 | tf_op jit(solution)/shard_map/ppermute | solution.py:410
  8.1 4.6 %shard_map.56 = (bf16[40,2,600,128]{3,2,1,0:T(8,128)(2,1)S(1)}, bf16[4,512,128]{2,1,0:T(8,128)(2,1)S(1)}) custom-call(bf16[8,32,128]{2,1,0:T(8,128)(2,1)S(1)} %get-tuple-element.24.after_ref.refs_0_, s32[1,424]{1,0:T(1,128)S(1)} %bitcast.4, bf16[106,2,600,128]{3,2,1,0:T(8,128)(2,1)} %refs_5_.3), custom_call_target="tpu_custom_call" | custom-call | flops 4000000000 | bytes 12288000 | tf_op jit(solution)/shard_map/pallas_call | solution.py:388
  13.2 6.4 %shard_map.57 = (f32[1216,128]{1,0:T(8,128)S(1)}, f32[1216,128]{1,0:T(8,128)S(1)}, bf16[24,2,600,128]{3,2,1,0:T(8,128)(2,1)S(1)}) custom-call(bf16[8,32,128]{2,1,0:T(8,128)(2,1)S(1)} %get-tuple-element.24.after_ref.refs_0_, bf16[8,32,128]{2,1,0:T(8,128)(2,1)S(1)} %collective-permute-done.refs_1_, bf16[8,32,128]{2,1,0:T(8,128)(2,1)S(1)} %collective-permute-done.1.refs_2_, ...), custom_call_target="tpu_custom_call" | custom-call | flops 2516582400 | bytes 19660800 | tf_op jit(solution)/shard_map/pallas_call | solution.py:388
  19.7 3.9 %shard_map.58 = (f32[1216,128]{1,0:T(8,128)S(1)}, f32[1216,128]{1,0:T(8,128)S(1)}) custom-call(bf16[8,32,128]{2,1,0:T(8,128)(2,1)S(1)} %get-tuple-element.24.after_ref.refs_0_, bf16[8,32,128]{2,1,0:T(8,128)(2,1)S(1)} %collective-permute-done.refs_1_, bf16[8,32,128]{2,1,0:T(8,128)(2,1)S(1)} %collective-permute-done.1.refs_2_, ...), custom_call_target="tpu_custom_call" | custom-call | flops 1651507200 | bytes 12902400 | tf_op jit(solution)/shard_map/pallas_call | solution.py:388
  23.6 0.5 collective-permute-start.4
  24.1 1.7 %collective-permute-done.4.refs_3_ = f32[1216,128]{1,0:T(8,128)S(1)} collective-permute-done((f32[1216,128]{1,0:T(8,128)S(1)}, f32[1216,128]{1,0:T(8,128)S(1)}, u32[]{:S(2)}, u32[]{:S(2)}) %collective-permute-start.4) | collective-permute-done | bytes 622624 | tf_op jit(solution)/shard_map/ppermute | solution.py:419
  26.0 1.5 %collective-permute-start.5 = (bf16[512,128]{1,0:T(8,128)(2,1)S(1)}, bf16[512,128]{1,0:T(8,128)(2,1)S(1)}, u32[]{:S(2)}, u32[]{:S(2)}) collective-permute-start(bf16[512,128]{1,0:T(8,128)(2,1)S(1)} %get-tuple-element.36), channel_id=1, source_target_pairs={{0,8},{8,0},{16,24},{24,16},{1,9},{9,1},{17,25},{25,17},{2,10},{10... | collective-permute-start | bytes 393224 | tf_op jit(solution)/shard_map/ppermute | solution.py:410
  27.5 1.5 %collective-permute-start.6 = (bf16[512,128]{1,0:T(8,128)(2,1)S(1)}, bf16[512,128]{1,0:T(8,128)(2,1)S(1)}, u32[]{:S(2)}, u32[]{:S(2)}) collective-permute-start(bf16[512,128]{1,0:T(8,128)(2,1)S(1)} %get-tuple-element.37), channel_id=1, source_target_pairs={{0,16},{8,24},{16,0},{24,8},{1,17},{9,25},{17,1},{25,9},{2,18},{10... | collective-permute-start | bytes 393224 | tf_op jit(solution)/shard_map/ppermute | solution.py:410
  29.5 2.7 %collective-permute-done.5.rest_1_ = bf16[512,128]{1,0:T(8,128)(2,1)S(1)} collective-permute-done((bf16[512,128]{1,0:T(8,128)(2,1)S(1)}, bf16[512,128]{1,0:T(8,128)(2,1)S(1)}, u32[]{:S(2)}, u32[]{:S(2)}) %collective-permute-start.5) | collective-permute-done | bytes 131104 | tf_op jit(solution)/shard_map/ppermute | solution.py:410
  32.3 3.5 %collective-permute-done.6.rest_2_ = bf16[512,128]{1,0:T(8,128)(2,1)S(1)} collective-permute-done((bf16[512,128]{1,0:T(8,128)(2,1)S(1)}, bf16[512,128]{1,0:T(8,128)(2,1)S(1)}, u32[]{:S(2)}, u32[]{:S(2)}) %collective-permute-start.6) | collective-permute-done | bytes 131104 | tf_op jit(solution)/shard_map/ppermute | solution.py:410
  35.8 2.0 %shard_map.60 = (f32[256,128]{1,0:T(8,128)S(1)}, bf16[256,128]{1,0:T(8,128)(2,1)S(1)}, bf16[256,128]{1,0:T(8,128)(2,1)S(1)}, bf16[256,128]{1,0:T(8,128)(2,1)S(1)}) custom-call(bf16[4,512,128]{2,1,0:T(8,128)(2,1)S(1)} %get-tuple-element.25.hits_ref, bf16[512,1024]{1,0:T(8,128)(2,1)S(1)} %copy-done.1, bf16[512,1024]{1,0:T(8,128)(2,1)S(1)} %copy-done, ...), custom_call_target="tpu_custom_call" | custom-call | tf_op jit(solution)/shard_map/pallas_call | solution.py:388
  37.8 1.6 %collective-permute-start.8 = (bf16[256,128]{1,0:T(8,128)(2,1)S(1)}, bf16[256,128]{1,0:T(8,128)(2,1)S(1)}, u32[]{:S(2)}, u32[]{:S(2)}) collective-permute-start(bf16[256,128]{1,0:T(8,128)(2,1)S(1)} %get-tuple-element.40), channel_id=1, source_target_pairs={{0,2},{1,3},{2,0},{3,1},{4,6},{5,7},{6,4},{7,5},{8,10},{9,11},{10,... | collective-permute-start | bytes 196616 | tf_op jit(solution)/shard_map/ppermute | solution.py:416
  39.4 2.6 %collective-permute-start.9 = (bf16[256,128]{1,0:T(8,128)(2,1)S(1)}, bf16[256,128]{1,0:T(8,128)(2,1)S(1)}, u32[]{:S(2)}, u32[]{:S(2)}) collective-permute-start(bf16[256,128]{1,0:T(8,128)(2,1)S(1)} %get-tuple-element.41), channel_id=1, source_target_pairs={{0,4},{1,5},{2,6},{3,7},{4,0},{5,1},{6,2},{7,3},{8,12},{9,13},{10,... | collective-permute-start | bytes 196616 | tf_op jit(solution)/shard_map/ppermute | solution.py:416
  42.7 3.2 %collective-permute-done.9.refs_2_ = bf16[256,128]{1,0:T(8,128)(2,1)S(1)} collective-permute-done((bf16[256,128]{1,0:T(8,128)(2,1)S(1)}, bf16[256,128]{1,0:T(8,128)(2,1)S(1)}, u32[]{:S(2)}, u32[]{:S(2)}) %collective-permute-start.9) | collective-permute-done | bytes 65568 | tf_op jit(solution)/shard_map/ppermute | solution.py:416
  46.0 2.2 %collective-permute-done.10.refs_3_ = bf16[256,128]{1,0:T(8,128)(2,1)S(1)} collective-permute-done((bf16[256,128]{1,0:T(8,128)(2,1)S(1)}, bf16[256,128]{1,0:T(8,128)(2,1)S(1)}, u32[]{:S(2)}, u32[]{:S(2)}) %collective-permute-start.10) | collective-permute-done | bytes 65568 | tf_op jit(solution)/shard_map/ppermute | solution.py:416
  48.2 1.1 %collective-permute-start.13 = (bf16[256,128]{1,0:T(8,128)(2,1)S(1)}, bf16[256,128]{1,0:T(8,128)(2,1)S(1)}, u32[]{:S(2)}, u32[]{:S(2)}) collective-permute-start(bf16[256,128]{1,0:T(8,128)(2,1)S(1)} %shard_map.61.refs_0_), channel_id=1, source_target_pairs={{0,6},{1,7},{2,4},{3,5},{4,2},{5,3},{6,0},{7,1},{8,14},{9,15},{10,... | collective-permute-start | bytes 196616 | tf_op jit(solution)/shard_map/ppermute | solution.py:416
  49.4 3.3 %collective-permute-start.11 = (bf16[256,128]{1,0:T(8,128)(2,1)S(1)}, bf16[256,128]{1,0:T(8,128)(2,1)S(1)}, u32[]{:S(2)}, u32[]{:S(2)}) collective-permute-start(bf16[256,128]{1,0:T(8,128)(2,1)S(1)} %shard_map.61.refs_0_), channel_id=1, source_target_pairs={{0,2},{1,3},{2,0},{3,1},{4,6},{5,7},{6,4},{7,5},{8,10},{9,11},{10,... | collective-permute-start | bytes 196616 | tf_op jit(solution)/shard_map/ppermute | solution.py:416
  52.7 1.8 %collective-permute-done.13.refs_3_ = bf16[256,128]{1,0:T(8,128)(2,1)S(1)} collective-permute-done((bf16[256,128]{1,0:T(8,128)(2,1)S(1)}, bf16[256,128]{1,0:T(8,128)(2,1)S(1)}, u32[]{:S(2)}, u32[]{:S(2)}) %collective-permute-start.13) | collective-permute-done | bytes 65568 | tf_op jit(solution)/shard_map/ppermute | solution.py:416
  54.4 1.3 %collective-permute-done.12.refs_2_ = bf16[256,128]{1,0:T(8,128)(2,1)S(1)} collective-permute-done((bf16[256,128]{1,0:T(8,128)(2,1)S(1)}, bf16[256,128]{1,0:T(8,128)(2,1)S(1)}, u32[]{:S(2)}, u32[]{:S(2)}) %collective-permute-start.12) | collective-permute-done | bytes 65568 | tf_op jit(solution)/shard_map/ppermute | solution.py:416
  55.8 1.5 %collective-permute-done.14.refs_1_ = bf16[1024,128]{1,0:T(8,128)(2,1)S(1)} collective-permute-done((bf16[1024,128]{1,0:T(8,128)(2,1)S(1)}, bf16[1024,128]{1,0:T(8,128)(2,1)S(1)}, u32[]{:S(2)}, u32[]{:S(2)}) %collective-permute-start.14) | collective-permute-done | bytes 262176 | tf_op jit(solution)/shard_map/ppermute | solution.py:419
  57.4 1.7 %shard_map.63 = f32[150,4,420]{2,1,0:T(4,128)} custom-call(bf16[1024,128]{1,0:T(8,128)(2,1)S(1)} %shard_map.62.refs_0_, bf16[1024,128]{1,0:T(8,128)(2,1)S(1)} %collective-permute-done.14.refs_1_), custom_call_target="tpu_custom_call" | custom-call | tf_op jit(solution)/shard_map/pallas_call | solution.py:388
  (21 shorter events, 2.2 us)
Async XLA Ops:
  0.0 0.7 %copy-start.2 = (s32[424]{0:T(512)S(1)}, s32[424]{0:T(512)}, u32[]{:S(2)}) copy-start(s32[424]{0:T(512)} %param.7) | copy-start | bytes 5092
  3.5 9.2 %collective-permute-start = (bf16[8,32,128]{2,1,0:T(8,128)(2,1)S(1)}, bf16[8,32,128]{2,1,0:T(8,128)(2,1)S(1)}, u32[]{:S(2)}, u32[]{:S(2)}) collective-permute-start(bf16[8,32,128]{2,1,0:T(8,128)(2,1)S(1)} %get-tuple-element.26), channel_id=1, source_target_pairs={{0,8},{8,0},{16,24},{24,16},{1,9},{9,1},{17,25},{25,17},{2,10},{10... | collective-permute-start | bytes 196616 | tf_op jit(solution)/shard_map/ppermute | solution.py:410
  6.5 6.2 %collective-permute-start.1 = (bf16[8,32,128]{2,1,0:T(8,128)(2,1)S(1)}, bf16[8,32,128]{2,1,0:T(8,128)(2,1)S(1)}, u32[]{:S(2)}, u32[]{:S(2)}) collective-permute-start(bf16[8,32,128]{2,1,0:T(8,128)(2,1)S(1)} %get-tuple-element.27), channel_id=1, source_target_pairs={{0,16},{8,24},{16,0},{24,8},{1,17},{9,25},{17,1},{25,9},{2,18},{10... | collective-permute-start | bytes 196616 | tf_op jit(solution)/shard_map/ppermute | solution.py:410
  8.1 5.2 %collective-permute-start.2 = (bf16[8,32,128]{2,1,0:T(8,128)(2,1)S(1)}, bf16[8,32,128]{2,1,0:T(8,128)(2,1)S(1)}, u32[]{:S(2)}, u32[]{:S(2)}) collective-permute-start(bf16[8,32,128]{2,1,0:T(8,128)(2,1)S(1)} %get-tuple-element.28), channel_id=1, source_target_pairs={{0,24},{8,16},{16,8},{24,0},{1,25},{9,17},{17,9},{25,1},{2,26},{10... | collective-permute-start | bytes 196616 | tf_op jit(solution)/shard_map/ppermute | solution.py:410
  19.6 4.5 %collective-permute-start.3 = (f32[1216,128]{1,0:T(8,128)S(1)}, f32[1216,128]{1,0:T(8,128)S(1)}, u32[]{:S(2)}, u32[]{:S(2)}) collective-permute-start(f32[1216,128]{1,0:T(8,128)S(1)} %get-tuple-element.31), channel_id=1, source_target_pairs={{0,1},{1,0},{2,3},{3,2},{4,5},{5,4},{6,7},{7,6},{8,9},{9,8},{10,11... | collective-permute-start | bytes 1867784 | tf_op jit(solution)/shard_map/ppermute | solution.py:419
  19.7 16.1 %copy-start = (bf16[512,1024]{1,0:T(8,128)(2,1)S(1)}, bf16[512,1024]{1,0:T(8,128)(2,1)}, u32[]{:S(2)}) copy-start(bf16[512,1024]{1,0:T(8,128)(2,1)} %constant.5.clone.refs_3_.low_ref) | copy-start | bytes 3145732
  19.7 16.1 %copy-start.1 = (bf16[512,1024]{1,0:T(8,128)(2,1)S(1)}, bf16[512,1024]{1,0:T(8,128)(2,1)}, u32[]{:S(2)}) copy-start(bf16[512,1024]{1,0:T(8,128)(2,1)} %constant.4.clone.refs_2_.high_ref) | copy-start | bytes 3145732
  23.6 2.2 %collective-permute-start.4 = (f32[1216,128]{1,0:T(8,128)S(1)}, f32[1216,128]{1,0:T(8,128)S(1)}, u32[]{:S(2)}, u32[]{:S(2)}) collective-permute-start(f32[1216,128]{1,0:T(8,128)S(1)} %get-tuple-element.34), channel_id=1, source_target_pairs={{0,1},{1,0},{2,3},{3,2},{4,5},{5,4},{6,7},{7,6},{8,9},{9,8},{10,11... | collective-permute-start | bytes 1867784 | tf_op jit(solution)/shard_map/ppermute | solution.py:419
  26.0 6.3 %collective-permute-start.5 = (bf16[512,128]{1,0:T(8,128)(2,1)S(1)}, bf16[512,128]{1,0:T(8,128)(2,1)S(1)}, u32[]{:S(2)}, u32[]{:S(2)}) collective-permute-start(bf16[512,128]{1,0:T(8,128)(2,1)S(1)} %get-tuple-element.36), channel_id=1, source_target_pairs={{0,8},{8,0},{16,24},{24,16},{1,9},{9,1},{17,25},{25,17},{2,10},{10... | collective-permute-start | bytes 393224 | tf_op jit(solution)/shard_map/ppermute | solution.py:410
  27.5 8.3 %collective-permute-start.6 = (bf16[512,128]{1,0:T(8,128)(2,1)S(1)}, bf16[512,128]{1,0:T(8,128)(2,1)S(1)}, u32[]{:S(2)}, u32[]{:S(2)}) collective-permute-start(bf16[512,128]{1,0:T(8,128)(2,1)S(1)} %get-tuple-element.37), channel_id=1, source_target_pairs={{0,16},{8,24},{16,0},{24,8},{1,17},{9,25},{17,1},{25,9},{2,18},{10... | collective-permute-start | bytes 393224 | tf_op jit(solution)/shard_map/ppermute | solution.py:410
  29.0 6.8 %collective-permute-start.7 = (bf16[512,128]{1,0:T(8,128)(2,1)S(1)}, bf16[512,128]{1,0:T(8,128)(2,1)S(1)}, u32[]{:S(2)}, u32[]{:S(2)}) collective-permute-start(bf16[512,128]{1,0:T(8,128)(2,1)S(1)} %get-tuple-element.38), channel_id=1, source_target_pairs={{0,24},{8,16},{16,8},{24,0},{1,25},{9,17},{17,9},{25,1},{2,26},{10... | collective-permute-start | bytes 393224 | tf_op jit(solution)/shard_map/ppermute | solution.py:410
  37.8 5.0 %collective-permute-start.8 = (bf16[256,128]{1,0:T(8,128)(2,1)S(1)}, bf16[256,128]{1,0:T(8,128)(2,1)S(1)}, u32[]{:S(2)}, u32[]{:S(2)}) collective-permute-start(bf16[256,128]{1,0:T(8,128)(2,1)S(1)} %get-tuple-element.40), channel_id=1, source_target_pairs={{0,2},{1,3},{2,0},{3,1},{4,6},{5,7},{6,4},{7,5},{8,10},{9,11},{10,... | collective-permute-start | bytes 196616 | tf_op jit(solution)/shard_map/ppermute | solution.py:416
  39.4 6.6 %collective-permute-start.9 = (bf16[256,128]{1,0:T(8,128)(2,1)S(1)}, bf16[256,128]{1,0:T(8,128)(2,1)S(1)}, u32[]{:S(2)}, u32[]{:S(2)}) collective-permute-start(bf16[256,128]{1,0:T(8,128)(2,1)S(1)} %get-tuple-element.41), channel_id=1, source_target_pairs={{0,4},{1,5},{2,6},{3,7},{4,0},{5,1},{6,2},{7,3},{8,12},{9,13},{10,... | collective-permute-start | bytes 196616 | tf_op jit(solution)/shard_map/ppermute | solution.py:416
  42.0 6.2 %collective-permute-start.10 = (bf16[256,128]{1,0:T(8,128)(2,1)S(1)}, bf16[256,128]{1,0:T(8,128)(2,1)S(1)}, u32[]{:S(2)}, u32[]{:S(2)}) collective-permute-start(bf16[256,128]{1,0:T(8,128)(2,1)S(1)} %get-tuple-element.42), channel_id=1, source_target_pairs={{0,6},{1,7},{2,4},{3,5},{4,2},{5,3},{6,0},{7,1},{8,14},{9,15},{10,... | collective-permute-start | bytes 196616 | tf_op jit(solution)/shard_map/ppermute | solution.py:416
  48.2 6.2 %collective-permute-start.13 = (bf16[256,128]{1,0:T(8,128)(2,1)S(1)}, bf16[256,128]{1,0:T(8,128)(2,1)S(1)}, u32[]{:S(2)}, u32[]{:S(2)}) collective-permute-start(bf16[256,128]{1,0:T(8,128)(2,1)S(1)} %shard_map.61.refs_0_), channel_id=1, source_target_pairs={{0,6},{1,7},{2,4},{3,5},{4,2},{5,3},{6,0},{7,1},{8,14},{9,15},{10,... | collective-permute-start | bytes 196616 | tf_op jit(solution)/shard_map/ppermute | solution.py:416
  49.3 6.5 %collective-permute-start.12 = (bf16[256,128]{1,0:T(8,128)(2,1)S(1)}, bf16[256,128]{1,0:T(8,128)(2,1)S(1)}, u32[]{:S(2)}, u32[]{:S(2)}) collective-permute-start(bf16[256,128]{1,0:T(8,128)(2,1)S(1)} %shard_map.61.refs_0_), channel_id=1, source_target_pairs={{0,4},{1,5},{2,6},{3,7},{4,0},{5,1},{6,2},{7,3},{8,12},{9,13},{10,... | collective-permute-start | bytes 196616 | tf_op jit(solution)/shard_map/ppermute | solution.py:416
  49.4 6.4 %collective-permute-start.11 = (bf16[256,128]{1,0:T(8,128)(2,1)S(1)}, bf16[256,128]{1,0:T(8,128)(2,1)S(1)}, u32[]{:S(2)}, u32[]{:S(2)}) collective-permute-start(bf16[256,128]{1,0:T(8,128)(2,1)S(1)} %shard_map.61.refs_0_), channel_id=1, source_target_pairs={{0,2},{1,3},{2,0},{3,1},{4,6},{5,7},{6,4},{7,5},{8,10},{9,11},{10,... | collective-permute-start | bytes 196616 | tf_op jit(solution)/shard_map/ppermute | solution.py:416
  55.8 1.6 %collective-permute-start.14 = (bf16[1024,128]{1,0:T(8,128)(2,1)S(1)}, bf16[1024,128]{1,0:T(8,128)(2,1)S(1)}, u32[]{:S(2)}, u32[]{:S(2)}) collective-permute-start(bf16[1024,128]{1,0:T(8,128)(2,1)S(1)} %shard_map.62.refs_0_), channel_id=1, source_target_pairs={{0,1},{1,0},{2,3},{3,2},{4,5},{5,4},{6,7},{7,6},{8,9},{9,8},{10,11... | collective-permute-start | bytes 786440 | tf_op jit(solution)/shard_map/ppermute | solution.py:419

commit v2 on v1

--- a/solution.py
+++ b/solution.py
@@ -16,11 +16,15 @@
 LIMIT = 16 * MIB
 FULL = 67043328
 ROOM = 10 * MIB + 400 * 1024
-CHUNK, EARLY, AHEAD = 8, 5, 3
+CHUNK, EARLY, AHEAD = 8, 5, 2
 
 
 def up(value, unit):
     return -(-value // unit) * unit
+
+
+def by_step(refs):
+    return [refs[0], *refs[:0:-1]]
 
 
 def dot_nt(left, right):
@@ -57,7 +61,6 @@
         self.last = self.here - (self.groups - 1) * self.group
         self.fold = self.group // self.last
         self.fold_rows = up(-(-self.block_pad // self.fold), 8)
-        self.share_rows = (self.groups - 1) * self.block_pad + self.fold_rows
         self.rows = self.half * self.block_pad
         self.spare = self.span_pad - self.span
         self.base = self.rows
@@ -193,8 +196,10 @@
 
 def response_kernel(plan, begin, end, held, ahead, *refs):
     freq, group = plan.freq, plan.group
-    arrived, refs = refs[:freq], refs[freq:]
-    held_refs, kern_ref, refs = refs[: len(held)], refs[len(held)], refs[len(held) + 1 :]
+    arrived, refs = by_step(refs[:freq]), refs[freq:]
+    held_refs, refs = refs[: len(held)], refs[len(held) :]
+    if ahead or sum(held) < min(end * group, plan.here) - begin * group:
+        kern_ref, refs = refs[0], refs[1:]
     places = [(ref, at) for ref, size in zip(held_refs, held) for at in range(size)]
     ready = len(places)
     own_ref, other_ref, refs = refs[0], refs[1], refs[2:]
@@ -277,20 +282,23 @@
         copy.wait()
 
 
-def join_kernel(plan, sizes, *refs):
+def join_kernel(plan, sizes, last, *refs):
     pairs, outs = refs[: 2 * len(sizes)], refs[2 * len(sizes) :]
     me, pad, fold_rows = lax.axis_index("freq"), plan.block_pad, plan.fold_rows
     lane = lax.broadcasted_iota(I32, (fold_rows, LANES), 1) % plan.group
+    whole_groups = sum(sizes) - last
     for k in range(plan.freq):
         done = 0
         for call_at, size in enumerate(sizes):
             own_ref, other_ref = pairs[2 * call_at : 2 * call_at + 2]
             at = pl.multiple_of((me ^ k) * (size * pad), 8)
             value = own_ref[pl.ds(at, size * pad)] + other_ref[pl.ds(at, size * pad)]
-            full = min(size, plan.groups - 1 - done) * pad
+            full = min(size, whole_groups - done) * pad
             if full:
                 outs[k][done * pad : done * pad + full] = value[:full].astype(BF16)
             done += size
+        if not last:
+            continue
         tile, packed = value[full:], jnp.zeros((fold_rows, LANES), F32)
         for j in range(plan.fold):
             part = tile[j * fold_rows : (j + 1) * fold_rows]
@@ -300,20 +308,21 @@
             if j:
                 part = pltpu.roll(part, j * plan.last, 1)
             packed = jnp.where(lane // plan.last == j, part, packed)
-        outs[k][plan.share_rows - fold_rows :] = packed.astype(BF16)
+        outs[k][whole_groups * pad :] = packed.astype(BF16)
 
 
 def inverse_kernel(plan, hits_ref, high_ref, low_ref, *rest):
     freq, group, pad = plan.freq, plan.group, plan.block_pad
-    arrived, rest = rest[:freq], rest[freq:]
+    early, late, rest = by_step(rest[:freq]), by_step(rest[freq : 2 * freq]), rest[2 * freq :]
     outs, (joined_ref,) = rest[: plan.pieces], rest[plan.pieces :]
     me, piece = lax.axis_index("freq"), lax.axis_index("param") // 2
     lane = lax.broadcasted_iota(I32, (pad, LANES), 1)
     real_row = lax.broadcasted_iota(I32, (pad, LANES), 0) < plan.block
     for k in range(freq):
-        starts = range(0, (plan.groups - 1) * pad, pad)
-        tiles = [arrived[k][at : at + pad].astype(F32) for at in starts]
-        packed = arrived[k][plan.share_rows - plan.fold_rows :].astype(F32)
+        tiles = [early[k][at : at + pad].astype(F32) for at in range(0, early[k].shape[0], pad)]
+        whole_rows = late[k].shape[0] - plan.fold_rows
+        tiles += [late[k][at : at + pad].astype(F32) for at in range(0, whole_rows, pad)]
+        packed = late[k][whole_rows:].astype(F32)
         folds = [packed] + [
             pltpu.roll(packed, LANES - j * plan.last, 1) for j in range(1, plan.fold)
         ]
@@ -406,10 +415,11 @@
     whole = pl.BlockSpec(memory_space=VMEM)
 
     def over_freq(values):
-        return [values[0]] + [
-            lax.ppermute(values[k], "freq", [(i, i ^ k) for i in range(freq)])
-            for k in range(1, freq)
-        ]
+        moved = {
+            k: lax.ppermute(values[k], "freq", [(i, i ^ k) for i in range(freq)])
+            for k in range(freq - 1, 0, -1)
+        }
+        return [values[0], *moved.values()]
 
     def to_piece(value, k):
         pairs = [(2 * z + h, 2 * (z ^ k) + h) for z in range(pieces) for h in range(2)]
@@ -418,8 +428,8 @@
     def to_core(value):
         return lax.ppermute(value, "param", [(i, i ^ 1) for i in range(plan.param)])
 
-    middle = -(-plan.groups // 2)
-    ranges = [(0, middle), (middle, plan.groups)]
+    ends = [g for g in (plan.groups - 2, plan.groups - 1, plan.groups) if g > 0]
+    ranges = list(zip([0, *ends], ends))
     sizes = [end - begin for begin, end in ranges]
     totals = [min(end * plan.group, plan.here) - begin * plan.group for begin, end in ranges]
     block = (2, plan.sensors, plan.depth)
@@ -455,33 +465,41 @@
         cost=cost(4 * 10**9, 4 * early * plan.sensors * plan.depth),
     )
     ready = [ready]
+    def join(at, last):
+        groups = [sizes[i] for i in at]
+        rows = (sum(groups) - last) * plan.block_pad + last * plan.fold_rows
+        return call(
+            functools.partial(join_kernel, plan, groups, last),
+            [shape((rows, LANES), BF16)] * freq,
+            [array for i in at for array in pairs[2 * i : 2 * i + 2]],
+        )
+
     pairs = []
     for index, (begin, end) in enumerate(ranges):
         total, held = totals[index], [array.shape[0] for array in ready]
         rest = total - sum(held)
-        ahead = 0 if index else min(totals[1] // CHUNK, AHEAD) * CHUNK
+        ahead = min(totals[index + 1], AHEAD * CHUNK) if index + 1 < len(totals) else 0
+        streams = int(rest > 0 or ahead > 0)
         size = shape((freq * sizes[index] * plan.block_pad, LANES), F32)
         own, other, *later = call(
             functools.partial(response_kernel, plan, begin, end, held, ahead),
             [size, size] + ([shape((ahead, *block), BF16)] if ahead else []),
-            (*arrived, *ready, kernel),
-            in_specs=[whole] * (freq + len(ready)) + [hbm],
+            (*arrived, *ready) + (kernel,) * streams,
+            in_specs=[whole] * (freq + len(ready)) + [hbm] * streams,
             scratch=[
                 VMEM((max(rest, CHUNK), *block), BF16),
                 VMEM((2 * plan.count, plan.depth, LANES), BF16),
                 VMEM((end - begin, 2 * plan.depth, 2 * LANES), BF16),
-                pltpu.SemaphoreType.DMA((-(-rest // CHUNK) + ahead // CHUNK + 1,)),
+                pltpu.SemaphoreType.DMA((-(-rest // CHUNK) + -(-ahead // CHUNK) + 1,)),
             ],
             cost=cost(total * 512 * plan.sensors * plan.depth, 4 * total * plan.sensors * plan.depth),
         )
         ready = later
         pairs += [own, to_core(other)]
-    joined = call(
-        functools.partial(join_kernel, plan, sizes),
-        [shape((plan.share_rows, LANES), BF16)] * freq,
-        pairs,
-    )
-    parts = over_freq(joined)
+        if index == len(ranges) - 2:
+            joined, ready = lax.optimization_barrier((join([0], 0), ready))
+            parts = over_freq(joined)
+    parts += over_freq(join(list(range(1, len(sizes))), 1))
 
     partial = call(
         functools.partial(inverse_kernel, plan),
@@ -491,7 +509,7 @@
             VMEM((plan.comps * plan.block_pad, freq * LANES), BF16),
         ],
     )
-    received = [to_piece(partial[k], k) for k in range(1, pieces)]
+    received = [to_piece(partial[k], k) for k in range(pieces - 1, 0, -1)]
     piece = call(sum_kernel, shape((plan.base, plan.span_pad), BF16), (partial[0], *received))
     mine = [piece] + [to_piece(piece, k) for k in range(1, pieces)]
     mine = call(stack_kernel, shape((pieces * plan.base, plan.span_pad), BF16), mine)

time: 59.2 us -> 57.3 us (0.968)
  waiting for transfers between devices: 19 us -> 12.9 us
  starting transfers between devices: 17.7 us -> 21.9 us
    ppermute x6 -> x9, starting transfers between devices: 8.13 us -> 12.2 us  [over_freq(): lax.ppermute(values[k], 'freq', [(i, i ^ k) for i in range(freq)])]
    ppermute x6 -> x9, waiting for transfers between devices: 6.78 us -> 3.53 us  [over_freq(): lax.ppermute(values[k], 'freq', [(i, i ^ k) for i in range(freq)])]
    ppermute x3 -> x4, waiting for transfers between devices: 3.2 us -> 1.53 us  [to_core(): return lax.ppermute(value, 'param', [(i, i ^ 1) for i in range(plan.param)])]
    ppermute x6, waiting for transfers between devices: 9.03 us -> 7.86 us  [to_piece(): return lax.ppermute(value, 'param', pairs)]
    pallas_call x9 -> x11, Pallas kernels: 21.6 us -> 21.5 us  [call(): pl.pallas_call(body, out_shape=out_shapes, in_specs=in_specs or [whole] *...]
  transfers between devices with their start and end apart: 15 -> 19, of which waited for: 10 -> 9; matrix products, arithmetic and copies ran while one was open for 0% -> 0% of each run, Pallas kernels for 14% -> 16%
where the time goes in v2:
time: 57.3 us; the launch traced here: 57.2 us
  starting transfers between devices  21.9 us (38%)
  Pallas kernels  21.5 us (38%)
  waiting for transfers between devices  12.9 us (23%)
  local copies, waits for them, and re-layouts  0.69 us (1%)
    pallas_call x11, Pallas kernels, call(): pl.pallas_call(body, out_shape=out_shapes, in_specs=in_specs or [whole] *...  21.5 us
    ppermute x9, starting transfers between devices, over_freq(): lax.ppermute(values[k], 'freq', [(i, i ^ k) for i in range(freq)])  12.2 us
    ppermute x6, starting transfers between devices, to_piece(): return lax.ppermute(value, 'param', pairs)  8.91 us
    ppermute x6, waiting for transfers between devices, to_piece(): return lax.ppermute(value, 'param', pairs)  7.86 us
    ppermute x9, waiting for transfers between devices, over_freq(): lax.ppermute(values[k], 'freq', [(i, i ^ k) for i in range(freq)])  3.53 us
    ppermute x4, waiting for transfers between devices, to_core(): return lax.ppermute(value, 'param', [(i, i ^ 1) for i in range(plan.param)])  1.53 us
  transfers between devices with their start and end apart: 19, of which 9 were waited for; matrix products, arithmetic and copies ran while one was open for 0% of the time, Pallas kernels for 16%

profile of v2, /device:TPU:0, one launch (start us, length us, event | category | flops | bytes accessed | tf_op | source)
XLA Modules:
  0.0 57.2 jit_solution(2316302498353304808)
XLA Ops:
  0.0 0.7 %copy-done.2 = s32[424]{0:T(512)S(1)} copy-done((s32[424]{0:T(512)S(1)}, s32[424]{0:T(512)}, u32[]{:S(2)}) %copy-start.2) | copy-done | bytes 1720
  0.7 2.8 %shard_map.55 = (bf16[8,32,128]{2,1,0:T(8,128)(2,1)S(1)}, bf16[8,32,128]{2,1,0:T(8,128)(2,1)S(1)}, bf16[8,32,128]{2,1,0:T(8,128)(2,1)S(1)}, bf16[8,32,128]{2,1,0:T(8,128)(2,1)S(1)}) custom-call(s32[1,424]{1,0:T(1,128)S(1)} %bitcast.3, f32[4,32,420]{2,1,0:T(8,128)} %bitcast.5, bf16[512,1024]{1,0:T(8,128)(2,1)} %constant.4.clone.refs_2_.high_ref, ...), custom_call_target="tpu_custom_call" | custom-call | flops 2000000000 | bytes 1048576 | tf_op jit(solution)/shard_map/pallas_call | solution.py:397
  3.5 4.0 %collective-permute-start = (bf16[8,32,128]{2,1,0:T(8,128)(2,1)S(1)}, bf16[8,32,128]{2,1,0:T(8,128)(2,1)S(1)}, u32[]{:S(2)}, u32[]{:S(2)}) collective-permute-start(bf16[8,32,128]{2,1,0:T(8,128)(2,1)S(1)} %get-tuple-element.38), channel_id=1, source_target_pairs={{0,24},{8,16},{16,8},{24,0},{1,25},{9,17},{17,9},{25,1},{2,26},{10... | collective-permute-start | bytes 196616 | tf_op jit(solution)/shard_map/ppermute | solution.py:419
  8.1 4.6 %shard_map.56 = (bf16[40,2,600,128]{3,2,1,0:T(8,128)(2,1)S(1)}, bf16[4,512,128]{2,1,0:T(8,128)(2,1)S(1)}) custom-call(bf16[8,32,128]{2,1,0:T(8,128)(2,1)S(1)} %get-tuple-element.36.after_ref.refs_0_, s32[1,424]{1,0:T(1,128)S(1)} %bitcast.4, bf16[106,2,600,128]{3,2,1,0:T(8,128)(2,1)} %refs_5_.3), custom_call_target="tpu_custom_call" | custom-call | flops 4000000000 | bytes 12288000 | tf_op jit(solution)/shard_map/pallas_call | solution.py:397
  12.8 5.7 %shard_map.57 = (f32[1216,128]{1,0:T(8,128)S(1)}, f32[1216,128]{1,0:T(8,128)S(1)}, bf16[16,2,600,128]{3,2,1,0:T(8,128)(2,1)S(1)}) custom-call(bf16[8,32,128]{2,1,0:T(8,128)(2,1)S(1)} %get-tuple-element.36.after_ref.refs_0_, bf16[8,32,128]{2,1,0:T(8,128)(2,1)S(1)} %collective-permute-done.refs_1_, bf16[8,32,128]{2,1,0:T(8,128)(2,1)S(1)} %collective-permute-done.1.refs_2_, ...), custom_call_target="tpu_custom_call" | custom-call | flops 2516582400 | bytes 19660800 | tf_op jit(solution)/shard_map/pallas_call | solution.py:397
  18.6 3.3 %shard_map.59 = (f32[608,128]{1,0:T(8,128)S(1)}, f32[608,128]{1,0:T(8,128)S(1)}, bf16[10,2,600,128]{3,2,1,0:T(8,128)(2,1)S(1)}) custom-call(bf16[8,32,128]{2,1,0:T(8,128)(2,1)S(1)} %get-tuple-element.36.after_ref.refs_0_, bf16[8,32,128]{2,1,0:T(8,128)(2,1)S(1)} %collective-permute-done.refs_1_, bf16[8,32,128]{2,1,0:T(8,128)(2,1)S(1)} %collective-permute-done.1.refs_2_, ...), custom_call_target="tpu_custom_call" | custom-call | flops 1258291200 | bytes 9830400 | tf_op jit(solution)/shard_map/pallas_call | solution.py:397
  22.6 1.1 %shard_map.60 = (f32[608,128]{1,0:T(8,128)S(1)}, f32[608,128]{1,0:T(8,128)S(1)}) custom-call(bf16[8,32,128]{2,1,0:T(8,128)(2,1)S(1)} %get-tuple-element.36.after_ref.refs_0_, bf16[8,32,128]{2,1,0:T(8,128)(2,1)S(1)} %collective-permute-done.refs_1_, bf16[8,32,128]{2,1,0:T(8,128)(2,1)S(1)} %collective-permute-done.1.refs_2_, ...), custom_call_target="tpu_custom_call" | custom-call | flops 393216000 | bytes 3072000 | tf_op jit(solution)/shard_map/pallas_call | solution.py:397
  23.8 2.9 %collective-permute-start.4 = (bf16[304,128]{1,0:T(8,128)(2,1)S(1)}, bf16[304,128]{1,0:T(8,128)(2,1)S(1)}, u32[]{:S(2)}, u32[]{:S(2)}) collective-permute-start(bf16[304,128]{1,0:T(8,128)(2,1)S(1)} %get-tuple-element.51), channel_id=1, source_target_pairs={{0,24},{8,16},{16,8},{24,0},{1,25},{9,17},{17,9},{25,1},{2,26},{10... | collective-permute-start | bytes 233480 | tf_op jit(solution)/shard_map/ppermute | solution.py:419
  27.5 2.9 %collective-permute-start.9 = (bf16[208,128]{1,0:T(8,128)(2,1)S(1)}, bf16[208,128]{1,0:T(8,128)(2,1)S(1)}, u32[]{:S(2)}, u32[]{:S(2)}) collective-permute-start(bf16[208,128]{1,0:T(8,128)(2,1)S(1)} %get-tuple-element.60), channel_id=1, source_target_pairs={{0,24},{8,16},{16,8},{24,0},{1,25},{9,17},{17,9},{25,1},{2,26},{10... | collective-permute-start | bytes 159752 | tf_op jit(solution)/shard_map/ppermute | solution.py:419
  30.9 0.6 %collective-permute-start.11 = (bf16[208,128]{1,0:T(8,128)(2,1)S(1)}, bf16[208,128]{1,0:T(8,128)(2,1)S(1)}, u32[]{:S(2)}, u32[]{:S(2)}) collective-permute-start(bf16[208,128]{1,0:T(8,128)(2,1)S(1)} %get-tuple-element.62), channel_id=1, source_target_pairs={{0,8},{8,0},{16,24},{24,16},{1,9},{9,1},{17,25},{25,17},{2,10},{10... | collective-permute-start | bytes 159752 | tf_op jit(solution)/shard_map/ppermute | solution.py:419
  31.5 0.6 %collective-permute-done.6.rest_3_ = bf16[304,128]{1,0:T(8,128)(2,1)S(1)} collective-permute-done((bf16[304,128]{1,0:T(8,128)(2,1)S(1)}, bf16[304,128]{1,0:T(8,128)(2,1)S(1)}, u32[]{:S(2)}, u32[]{:S(2)}) %collective-permute-start.6) | collective-permute-done | bytes 77856 | tf_op jit(solution)/shard_map/ppermute | solution.py:419
  32.1 1.3 %collective-permute-done.9.rest_5_ = bf16[208,128]{1,0:T(8,128)(2,1)S(1)} collective-permute-done((bf16[208,128]{1,0:T(8,128)(2,1)S(1)}, bf16[208,128]{1,0:T(8,128)(2,1)S(1)}, u32[]{:S(2)}, u32[]{:S(2)}) %collective-permute-start.9) | collective-permute-done | bytes 53280 | tf_op jit(solution)/shard_map/ppermute | solution.py:419
  33.5 1.1 %collective-permute-done.10.rest_6_ = bf16[208,128]{1,0:T(8,128)(2,1)S(1)} collective-permute-done((bf16[208,128]{1,0:T(8,128)(2,1)S(1)}, bf16[208,128]{1,0:T(8,128)(2,1)S(1)}, u32[]{:S(2)}, u32[]{:S(2)}) %collective-permute-start.10) | collective-permute-done | bytes 53280 | tf_op jit(solution)/shard_map/ppermute | solution.py:419
  35.0 2.0 %shard_map.62 = (f32[256,128]{1,0:T(8,128)S(1)}, bf16[256,128]{1,0:T(8,128)(2,1)S(1)}, bf16[256,128]{1,0:T(8,128)(2,1)S(1)}, bf16[256,128]{1,0:T(8,128)(2,1)S(1)}) custom-call(bf16[4,512,128]{2,1,0:T(8,128)(2,1)S(1)} %get-tuple-element.37.hits_ref, bf16[512,1024]{1,0:T(8,128)(2,1)S(1)} %copy-done.1, bf16[512,1024]{1,0:T(8,128)(2,1)S(1)} %copy-done, ...), custom_call_target="tpu_custom_call" | custom-call | tf_op jit(solution)/shard_map/pallas_call | solution.py:397
  37.0 3.7 %collective-permute-start.12 = (bf16[256,128]{1,0:T(8,128)(2,1)S(1)}, bf16[256,128]{1,0:T(8,128)(2,1)S(1)}, u32[]{:S(2)}, u32[]{:S(2)}) collective-permute-start(bf16[256,128]{1,0:T(8,128)(2,1)S(1)} %get-tuple-element.64), channel_id=1, source_target_pairs={{0,6},{1,7},{2,4},{3,5},{4,2},{5,3},{6,0},{7,1},{8,14},{9,15},{10,... | collective-permute-start | bytes 196616 | tf_op jit(solution)/shard_map/ppermute | solution.py:426
  40.7 0.8 %collective-permute-start.14 = (bf16[256,128]{1,0:T(8,128)(2,1)S(1)}, bf16[256,128]{1,0:T(8,128)(2,1)S(1)}, u32[]{:S(2)}, u32[]{:S(2)}) collective-permute-start(bf16[256,128]{1,0:T(8,128)(2,1)S(1)} %get-tuple-element.66), channel_id=1, source_target_pairs={{0,2},{1,3},{2,0},{3,1},{4,6},{5,7},{6,4},{7,5},{8,10},{9,11},{10,... | collective-permute-start | bytes 196616 | tf_op jit(solution)/shard_map/ppermute | solution.py:426
  41.5 1.7 %collective-permute-done.12.refs_1_ = bf16[256,128]{1,0:T(8,128)(2,1)S(1)} collective-permute-done((bf16[256,128]{1,0:T(8,128)(2,1)S(1)}, bf16[256,128]{1,0:T(8,128)(2,1)S(1)}, u32[]{:S(2)}, u32[]{:S(2)}) %collective-permute-start.12) | collective-permute-done | bytes 65568 | tf_op jit(solution)/shard_map/ppermute | solution.py:426
  43.2 2.7 %collective-permute-done.13.refs_2_ = bf16[256,128]{1,0:T(8,128)(2,1)S(1)} collective-permute-done((bf16[256,128]{1,0:T(8,128)(2,1)S(1)}, bf16[256,128]{1,0:T(8,128)(2,1)S(1)}, u32[]{:S(2)}, u32[]{:S(2)}) %collective-permute-start.13) | collective-permute-done | bytes 65568 | tf_op jit(solution)/shard_map/ppermute | solution.py:426
  45.9 2.1 %collective-permute-start.17 = (bf16[256,128]{1,0:T(8,128)(2,1)S(1)}, bf16[256,128]{1,0:T(8,128)(2,1)S(1)}, u32[]{:S(2)}, u32[]{:S(2)}) collective-permute-start(bf16[256,128]{1,0:T(8,128)(2,1)S(1)} %shard_map.63.refs_0_), channel_id=1, source_target_pairs={{0,6},{1,7},{2,4},{3,5},{4,2},{5,3},{6,0},{7,1},{8,14},{9,15},{10,... | collective-permute-start | bytes 196616 | tf_op jit(solution)/shard_map/ppermute | solution.py:426
  48.1 2.3 %collective-permute-start.15 = (bf16[256,128]{1,0:T(8,128)(2,1)S(1)}, bf16[256,128]{1,0:T(8,128)(2,1)S(1)}, u32[]{:S(2)}, u32[]{:S(2)}) collective-permute-start(bf16[256,128]{1,0:T(8,128)(2,1)S(1)} %shard_map.63.refs_0_), channel_id=1, source_target_pairs={{0,2},{1,3},{2,0},{3,1},{4,6},{5,7},{6,4},{7,5},{8,10},{9,11},{10,... | collective-permute-start | bytes 196616 | tf_op jit(solution)/shard_map/ppermute | solution.py:426
  50.4 1.7 %collective-permute-done.17.refs_3_ = bf16[256,128]{1,0:T(8,128)(2,1)S(1)} collective-permute-done((bf16[256,128]{1,0:T(8,128)(2,1)S(1)}, bf16[256,128]{1,0:T(8,128)(2,1)S(1)}, u32[]{:S(2)}, u32[]{:S(2)}) %collective-permute-start.17) | collective-permute-done | bytes 65568 | tf_op jit(solution)/shard_map/ppermute | solution.py:426
  52.0 1.8 %collective-permute-done.16.refs_2_ = bf16[256,128]{1,0:T(8,128)(2,1)S(1)} collective-permute-done((bf16[256,128]{1,0:T(8,128)(2,1)S(1)}, bf16[256,128]{1,0:T(8,128)(2,1)S(1)}, u32[]{:S(2)}, u32[]{:S(2)}) %collective-permute-start.16) | collective-permute-done | bytes 65568 | tf_op jit(solution)/shard_map/ppermute | solution.py:426
  53.9 1.5 %collective-permute-done.18.refs_1_ = bf16[1024,128]{1,0:T(8,128)(2,1)S(1)} collective-permute-done((bf16[1024,128]{1,0:T(8,128)(2,1)S(1)}, bf16[1024,128]{1,0:T(8,128)(2,1)S(1)}, u32[]{:S(2)}, u32[]{:S(2)}) %collective-permute-start.18) | collective-permute-done | bytes 262176 | tf_op jit(solution)/shard_map/ppermute | solution.py:429
  55.5 1.7 %shard_map.65 = f32[150,4,420]{2,1,0:T(4,128)} custom-call(bf16[1024,128]{1,0:T(8,128)(2,1)S(1)} %shard_map.64.refs_0_, bf16[1024,128]{1,0:T(8,128)(2,1)S(1)} %collective-permute-done.18.refs_1_), custom_call_target="tpu_custom_call" | custom-call | tf_op jit(solution)/shard_map/pallas_call | solution.py:397
  (31 shorter events, 3.5 us)
Async XLA Ops:
  0.0 0.7 %copy-start.2 = (s32[424]{0:T(512)S(1)}, s32[424]{0:T(512)}, u32[]{:S(2)}) copy-start(s32[424]{0:T(512)} %param.7) | copy-start | bytes 5092
  3.5 9.3 %collective-permute-start = (bf16[8,32,128]{2,1,0:T(8,128)(2,1)S(1)}, bf16[8,32,128]{2,1,0:T(8,128)(2,1)S(1)}, u32[]{:S(2)}, u32[]{:S(2)}) collective-permute-start(bf16[8,32,128]{2,1,0:T(8,128)(2,1)S(1)} %get-tuple-element.38), channel_id=1, source_target_pairs={{0,24},{8,16},{16,8},{24,0},{1,25},{9,17},{17,9},{25,1},{2,26},{10... | collective-permute-start | bytes 196616 | tf_op jit(solution)/shard_map/ppermute | solution.py:419
  7.5 5.3 %collective-permute-start.1 = (bf16[8,32,128]{2,1,0:T(8,128)(2,1)S(1)}, bf16[8,32,128]{2,1,0:T(8,128)(2,1)S(1)}, u32[]{:S(2)}, u32[]{:S(2)}) collective-permute-start(bf16[8,32,128]{2,1,0:T(8,128)(2,1)S(1)} %get-tuple-element.39), channel_id=1, source_target_pairs={{0,16},{8,24},{16,0},{24,8},{1,17},{9,25},{17,1},{25,9},{2,18},{10... | collective-permute-start | bytes 196616 | tf_op jit(solution)/shard_map/ppermute | solution.py:419
  8.0 4.8 %collective-permute-start.2 = (bf16[8,32,128]{2,1,0:T(8,128)(2,1)S(1)}, bf16[8,32,128]{2,1,0:T(8,128)(2,1)S(1)}, u32[]{:S(2)}, u32[]{:S(2)}) collective-permute-start(bf16[8,32,128]{2,1,0:T(8,128)(2,1)S(1)} %get-tuple-element.40), channel_id=1, source_target_pairs={{0,8},{8,0},{16,24},{24,16},{1,9},{9,1},{17,25},{25,17},{2,10},{10... | collective-permute-start | bytes 196616 | tf_op jit(solution)/shard_map/ppermute | solution.py:419
  18.5 4.0 %collective-permute-start.3 = (f32[1216,128]{1,0:T(8,128)S(1)}, f32[1216,128]{1,0:T(8,128)S(1)}, u32[]{:S(2)}, u32[]{:S(2)}) collective-permute-start(f32[1216,128]{1,0:T(8,128)S(1)} %get-tuple-element.43), channel_id=1, source_target_pairs={{0,1},{1,0},{2,3},{3,2},{4,5},{5,4},{6,7},{7,6},{8,9},{9,8},{10,11... | collective-permute-start | bytes 1867784 | tf_op jit(solution)/shard_map/ppermute | solution.py:429
  21.9 13.1 %copy-start = (bf16[512,1024]{1,0:T(8,128)(2,1)S(1)}, bf16[512,1024]{1,0:T(8,128)(2,1)}, u32[]{:S(2)}) copy-start(bf16[512,1024]{1,0:T(8,128)(2,1)} %constant.5.clone.refs_3_.low_ref) | copy-start | bytes 3145732
  21.9 13.1 %copy-start.1 = (bf16[512,1024]{1,0:T(8,128)(2,1)S(1)}, bf16[512,1024]{1,0:T(8,128)(2,1)}, u32[]{:S(2)}) copy-start(bf16[512,1024]{1,0:T(8,128)(2,1)} %constant.4.clone.refs_2_.high_ref) | copy-start | bytes 3145732
  21.9 5.4 %collective-permute-start.7 = (f32[608,128]{1,0:T(8,128)S(1)}, f32[608,128]{1,0:T(8,128)S(1)}, u32[]{:S(2)}, u32[]{:S(2)}) collective-permute-start(f32[608,128]{1,0:T(8,128)S(1)} %get-tuple-element.55), channel_id=1, source_target_pairs={{0,1},{1,0},{2,3},{3,2},{4,5},{5,4},{6,7},{7,6},{8,9},{9,8},{10,11... | collective-permute-start | bytes 933896 | tf_op jit(solution)/shard_map/ppermute | solution.py:429
  23.7 3.6 %collective-permute-start.8 = (f32[608,128]{1,0:T(8,128)S(1)}, f32[608,128]{1,0:T(8,128)S(1)}, u32[]{:S(2)}, u32[]{:S(2)}) collective-permute-start(f32[608,128]{1,0:T(8,128)S(1)} %get-tuple-element.58), channel_id=1, source_target_pairs={{0,1},{1,0},{2,3},{3,2},{4,5},{5,4},{6,7},{7,6},{8,9},{9,8},{10,11... | collective-permute-start | bytes 933896 | tf_op jit(solution)/shard_map/ppermute | solution.py:429
  23.8 7.1 %collective-permute-start.4 = (bf16[304,128]{1,0:T(8,128)(2,1)S(1)}, bf16[304,128]{1,0:T(8,128)(2,1)S(1)}, u32[]{:S(2)}, u32[]{:S(2)}) collective-permute-start(bf16[304,128]{1,0:T(8,128)(2,1)S(1)} %get-tuple-element.51), channel_id=1, source_target_pairs={{0,24},{8,16},{16,8},{24,0},{1,25},{9,17},{17,9},{25,1},{2,26},{10... | collective-permute-start | bytes 233480 | tf_op jit(solution)/shard_map/ppermute | solution.py:419
  26.7 4.8 %collective-permute-start.5 = (bf16[304,128]{1,0:T(8,128)(2,1)S(1)}, bf16[304,128]{1,0:T(8,128)(2,1)S(1)}, u32[]{:S(2)}, u32[]{:S(2)}) collective-permute-start(bf16[304,128]{1,0:T(8,128)(2,1)S(1)} %get-tuple-element.52), channel_id=1, source_target_pairs={{0,16},{8,24},{16,0},{24,8},{1,17},{9,25},{17,1},{25,9},{2,18},{10... | collective-permute-start | bytes 233480 | tf_op jit(solution)/shard_map/ppermute | solution.py:419
  27.2 4.9 %collective-permute-start.6 = (bf16[304,128]{1,0:T(8,128)(2,1)S(1)}, bf16[304,128]{1,0:T(8,128)(2,1)S(1)}, u32[]{:S(2)}, u32[]{:S(2)}) collective-permute-start(bf16[304,128]{1,0:T(8,128)(2,1)S(1)} %get-tuple-element.53), channel_id=1, source_target_pairs={{0,8},{8,0},{16,24},{24,16},{1,9},{9,1},{17,25},{25,17},{2,10},{10... | collective-permute-start | bytes 233480 | tf_op jit(solution)/shard_map/ppermute | solution.py:419
  27.5 6.0 %collective-permute-start.9 = (bf16[208,128]{1,0:T(8,128)(2,1)S(1)}, bf16[208,128]{1,0:T(8,128)(2,1)S(1)}, u32[]{:S(2)}, u32[]{:S(2)}) collective-permute-start(bf16[208,128]{1,0:T(8,128)(2,1)S(1)} %get-tuple-element.60), channel_id=1, source_target_pairs={{0,24},{8,16},{16,8},{24,0},{1,25},{9,17},{17,9},{25,1},{2,26},{10... | collective-permute-start | bytes 159752 | tf_op jit(solution)/shard_map/ppermute | solution.py:419
  30.4 4.1 %collective-permute-start.10 = (bf16[208,128]{1,0:T(8,128)(2,1)S(1)}, bf16[208,128]{1,0:T(8,128)(2,1)S(1)}, u32[]{:S(2)}, u32[]{:S(2)}) collective-permute-start(bf16[208,128]{1,0:T(8,128)(2,1)S(1)} %get-tuple-element.61), channel_id=1, source_target_pairs={{0,16},{8,24},{16,0},{24,8},{1,17},{9,25},{17,1},{25,9},{2,18},{10... | collective-permute-start | bytes 159752 | tf_op jit(solution)/shard_map/ppermute | solution.py:419
  30.9 4.1 %collective-permute-start.11 = (bf16[208,128]{1,0:T(8,128)(2,1)S(1)}, bf16[208,128]{1,0:T(8,128)(2,1)S(1)}, u32[]{:S(2)}, u32[]{:S(2)}) collective-permute-start(bf16[208,128]{1,0:T(8,128)(2,1)S(1)} %get-tuple-element.62), channel_id=1, source_target_pairs={{0,8},{8,0},{16,24},{24,16},{1,9},{9,1},{17,25},{25,17},{2,10},{10... | collective-permute-start | bytes 159752 | tf_op jit(solution)/shard_map/ppermute | solution.py:419
  37.0 6.1 %collective-permute-start.12 = (bf16[256,128]{1,0:T(8,128)(2,1)S(1)}, bf16[256,128]{1,0:T(8,128)(2,1)S(1)}, u32[]{:S(2)}, u32[]{:S(2)}) collective-permute-start(bf16[256,128]{1,0:T(8,128)(2,1)S(1)} %get-tuple-element.64), channel_id=1, source_target_pairs={{0,6},{1,7},{2,4},{3,5},{4,2},{5,3},{6,0},{7,1},{8,14},{9,15},{10,... | collective-permute-start | bytes 196616 | tf_op jit(solution)/shard_map/ppermute | solution.py:426
  40.7 5.2 %collective-permute-start.13 = (bf16[256,128]{1,0:T(8,128)(2,1)S(1)}, bf16[256,128]{1,0:T(8,128)(2,1)S(1)}, u32[]{:S(2)}, u32[]{:S(2)}) collective-permute-start(bf16[256,128]{1,0:T(8,128)(2,1)S(1)} %get-tuple-element.65), channel_id=1, source_target_pairs={{0,4},{1,5},{2,6},{3,7},{4,0},{5,1},{6,2},{7,3},{8,12},{9,13},{10,... | collective-permute-start | bytes 196616 | tf_op jit(solution)/shard_map/ppermute | solution.py:426
  40.7 5.2 %collective-permute-start.14 = (bf16[256,128]{1,0:T(8,128)(2,1)S(1)}, bf16[256,128]{1,0:T(8,128)(2,1)S(1)}, u32[]{:S(2)}, u32[]{:S(2)}) collective-permute-start(bf16[256,128]{1,0:T(8,128)(2,1)S(1)} %get-tuple-element.66), channel_id=1, source_target_pairs={{0,2},{1,3},{2,0},{3,1},{4,6},{5,7},{6,4},{7,5},{8,10},{9,11},{10,... | collective-permute-start | bytes 196616 | tf_op jit(solution)/shard_map/ppermute | solution.py:426
  45.9 6.1 %collective-permute-start.17 = (bf16[256,128]{1,0:T(8,128)(2,1)S(1)}, bf16[256,128]{1,0:T(8,128)(2,1)S(1)}, u32[]{:S(2)}, u32[]{:S(2)}) collective-permute-start(bf16[256,128]{1,0:T(8,128)(2,1)S(1)} %shard_map.63.refs_0_), channel_id=1, source_target_pairs={{0,6},{1,7},{2,4},{3,5},{4,2},{5,3},{6,0},{7,1},{8,14},{9,15},{10,... | collective-permute-start | bytes 196616 | tf_op jit(solution)/shard_map/ppermute | solution.py:426
  48.0 5.9 %collective-permute-start.16 = (bf16[256,128]{1,0:T(8,128)(2,1)S(1)}, bf16[256,128]{1,0:T(8,128)(2,1)S(1)}, u32[]{:S(2)}, u32[]{:S(2)}) collective-permute-start(bf16[256,128]{1,0:T(8,128)(2,1)S(1)} %shard_map.63.refs_0_), channel_id=1, source_target_pairs={{0,4},{1,5},{2,6},{3,7},{4,0},{5,1},{6,2},{7,3},{8,12},{9,13},{10,... | collective-permute-start | bytes 196616 | tf_op jit(solution)/shard_map/ppermute | solution.py:426
  48.1 5.8 %collective-permute-start.15 = (bf16[256,128]{1,0:T(8,128)(2,1)S(1)}, bf16[256,128]{1,0:T(8,128)(2,1)S(1)}, u32[]{:S(2)}, u32[]{:S(2)}) collective-permute-start(bf16[256,128]{1,0:T(8,128)(2,1)S(1)} %shard_map.63.refs_0_), channel_id=1, source_target_pairs={{0,2},{1,3},{2,0},{3,1},{4,6},{5,7},{6,4},{7,5},{8,10},{9,11},{10,... | collective-permute-start | bytes 196616 | tf_op jit(solution)/shard_map/ppermute | solution.py:426
  53.9 1.6 %collective-permute-start.18 = (bf16[1024,128]{1,0:T(8,128)(2,1)S(1)}, bf16[1024,128]{1,0:T(8,128)(2,1)S(1)}, u32[]{:S(2)}, u32[]{:S(2)}) collective-permute-start(bf16[1024,128]{1,0:T(8,128)(2,1)S(1)} %shard_map.64.refs_0_), channel_id=1, source_target_pairs={{0,1},{1,0},{2,3},{3,2},{4,5},{5,4},{6,7},{7,6},{8,9},{9,8},{10,11... | collective-permute-start | bytes 786440 | tf_op jit(solution)/shard_map/ppermute | solution.py:429

commit v3 on v2

--- a/solution.py
+++ b/solution.py
@@ -347,12 +347,16 @@
         rows.append(jnp.concatenate([real, imag], axis=1).astype(BF16))
     high = jnp.concatenate(rows, axis=0)
     scale = 1.0 / math.sqrt(2.0 * (plan.steps + 1))
-    for k in range(plan.pieces):
-        at = pl.multiple_of((piece ^ k) * plan.span_pad, plan.span_pad)
-        table_high = high_ref[pl.ds(at, plan.span_pad), :]
-        table_low = low_ref[pl.ds(at, plan.span_pad), :]
-        value = (dot_nt(high, table_high) + dot_nt(high, table_low)) * scale
-        outs[k][...] = pack(plan, value).astype(outs[k].dtype)
+    for pair in range(0, plan.pieces, 2):
+        at = [pl.multiple_of((piece ^ k) * plan.span_pad, plan.span_pad) for k in (pair, pair + 1)]
+        tables = [
+            jnp.concatenate([ref[pl.ds(i, plan.span_pad), :] for i in at], axis=0)
+            for ref in (high_ref, low_ref)
+        ]
+        value = (dot_nt(high, tables[0]) + dot_nt(high, tables[1])) * scale
+        for i in range(2):
+            half = value[:, i * plan.span_pad : (i + 1) * plan.span_pad]
+            outs[pair + i][...] = pack(plan, half).astype(outs[pair + i].dtype)
 
 
 def stack_kernel(*refs):
@@ -368,21 +372,29 @@
     refs[-1][...] = value.astype(BF16)
 
 
-def output_kernel(plan, *refs):
-    out_ref = refs[-1]
-    piece, core = lax.axis_index("param") // 2, lax.axis_index("param") % 2
-    width = plan.span_pad
+def by_time(plan, ref, pick):
+    parts = [
+        unpack(plan, ref[k * plan.base : (k + 1) * plan.base].astype(F32)).astype(BF16)
+        for k in range(plan.pieces)
+    ]
+    return dot_nt(jnp.concatenate(parts, axis=1), pick)
+
+
+def time_kernel(plan, ref, out_ref, pick_ref):
+    piece, width = lax.axis_index("param") // 2, plan.span_pad
     time = lax.broadcasted_iota(I32, (plan.steps, plan.pieces * width), 0)
     lane = lax.broadcasted_iota(I32, (plan.steps, plan.pieces * width), 1)
     inside = lane % width
     target = (lane // width ^ piece) * plan.span + inside
     pick = jnp.where((time == target) & (inside < plan.span), 1.0, 0.0).astype(BF16)
+    pick_ref[...] = pick
+    out_ref[...] = by_time(plan, ref, pick)
+
+
+def output_kernel(plan, mine_ref, theirs_ref, pick_ref, out_ref):
+    core = lax.axis_index("param") % 2
     for side in range(2):
-        parts = [
-            unpack(plan, refs[side][k * plan.base : (k + 1) * plan.base].astype(F32)).astype(BF16)
-            for k in range(plan.pieces)
-        ]
-        value = dot_nt(jnp.concatenate(parts, axis=1), pick)
+        value = by_time(plan, theirs_ref, pick_ref[...]) if side else mine_ref[...]
         for c in range(plan.half):
             at = c * plan.block_pad
             out_ref[:, (core ^ side) * plan.half + c, :] = value[at : at + plan.block]
@@ -514,10 +526,19 @@
     mine = [piece] + [to_piece(piece, k) for k in range(1, pieces)]
     mine = call(stack_kernel, shape((pieces * plan.base, plan.span_pad), BF16), mine)
     theirs = to_core(mine)
+    ours, pick = call(
+        functools.partial(time_kernel, plan),
+        [
+            shape((plan.rows, plan.steps), F32),
+            shape((plan.steps, pieces * plan.span_pad), BF16),
+        ],
+        (mine,),
+        cost=cost(10**9, 10**6),
+    )
     by_sensor = call(
         functools.partial(output_kernel, plan),
         shape((plan.block, plan.count, plan.steps), F32),
-        (mine, theirs),
+        (ours, theirs, pick),
     )
     return jnp.transpose(by_sensor, (1, 2, 0))
 

time: 57.3 us -> 56.4 us (0.984)
    pallas_call x11 -> x12, Pallas kernels: 21.5 us -> 21 us  [call(): pl.pallas_call(body, out_shape=out_shapes, in_specs=in_specs or [whole] *...]
  transfers between devices with their start and end apart: 19 -> 19, of which waited for: 9 -> 9; matrix products, arithmetic and copies ran while one was open for 0% -> 0% of each run, Pallas kernels for 16% -> 17%
where the time goes in v3:
time: 56.4 us; the launch traced here: 56.3 us
  starting transfers between devices  21.9 us (39%)
  Pallas kernels  21 us (37%)
  waiting for transfers between devices  12.5 us (22%)
  local copies, waits for them, and re-layouts  0.69 us (1%)
    pallas_call x12, Pallas kernels, call(): pl.pallas_call(body, out_shape=out_shapes, in_specs=in_specs or [whole] *...  21 us
    ppermute x9, starting transfers between devices, over_freq(): lax.ppermute(values[k], 'freq', [(i, i ^ k) for i in range(freq)])  12.2 us
    ppermute x6, starting transfers between devices, to_piece(): return lax.ppermute(value, 'param', pairs)  8.91 us
    ppermute x6, waiting for transfers between devices, to_piece(): return lax.ppermute(value, 'param', pairs)  7.86 us
    ppermute x9, waiting for transfers between devices, over_freq(): lax.ppermute(values[k], 'freq', [(i, i ^ k) for i in range(freq)])  3.53 us
  transfers between devices with their start and end apart: 19, of which 9 were waited for; matrix products, arithmetic and copies ran while one was open for 0% of the time, Pallas kernels for 17%

profile of v3, /device:TPU:0, one launch (start us, length us, event | category | flops | bytes accessed | tf_op | source)
XLA Modules:
  0.0 56.3 jit_solution(2507387620602193888)
XLA Ops:
  0.0 0.7 %copy-done.2 = s32[424]{0:T(512)S(1)} copy-done((s32[424]{0:T(512)S(1)}, s32[424]{0:T(512)}, u32[]{:S(2)}) %copy-start.2) | copy-done | bytes 1720
  0.7 2.8 %shard_map.55 = (bf16[8,32,128]{2,1,0:T(8,128)(2,1)S(1)}, bf16[8,32,128]{2,1,0:T(8,128)(2,1)S(1)}, bf16[8,32,128]{2,1,0:T(8,128)(2,1)S(1)}, bf16[8,32,128]{2,1,0:T(8,128)(2,1)S(1)}) custom-call(s32[1,424]{1,0:T(1,128)S(1)} %bitcast.3, f32[4,32,420]{2,1,0:T(8,128)} %bitcast.5, bf16[512,1024]{1,0:T(8,128)(2,1)} %constant.4.clone.refs_2_.high_ref, ...), custom_call_target="tpu_custom_call" | custom-call | flops 2000000000 | bytes 1048576 | tf_op jit(solution)/shard_map/pallas_call | solution.py:409
  3.5 4.0 %collective-permute-start = (bf16[8,32,128]{2,1,0:T(8,128)(2,1)S(1)}, bf16[8,32,128]{2,1,0:T(8,128)(2,1)S(1)}, u32[]{:S(2)}, u32[]{:S(2)}) collective-permute-start(bf16[8,32,128]{2,1,0:T(8,128)(2,1)S(1)} %get-tuple-element.40), channel_id=1, source_target_pairs={{0,24},{8,16},{16,8},{24,0},{1,25},{9,17},{17,9},{25,1},{2,26},{10... | collective-permute-start | bytes 196616 | tf_op jit(solution)/shard_map/ppermute | solution.py:431
  8.1 4.6 %shard_map.56 = (bf16[40,2,600,128]{3,2,1,0:T(8,128)(2,1)S(1)}, bf16[4,512,128]{2,1,0:T(8,128)(2,1)S(1)}) custom-call(bf16[8,32,128]{2,1,0:T(8,128)(2,1)S(1)} %get-tuple-element.38.after_ref.refs_0_, s32[1,424]{1,0:T(1,128)S(1)} %bitcast.4, bf16[106,2,600,128]{3,2,1,0:T(8,128)(2,1)} %refs_5_.3), custom_call_target="tpu_custom_call" | custom-call | flops 4000000000 | bytes 12288000 | tf_op jit(solution)/shard_map/pallas_call | solution.py:409
  12.8 5.7 %shard_map.57 = (f32[1216,128]{1,0:T(8,128)S(1)}, f32[1216,128]{1,0:T(8,128)S(1)}, bf16[16,2,600,128]{3,2,1,0:T(8,128)(2,1)S(1)}) custom-call(bf16[8,32,128]{2,1,0:T(8,128)(2,1)S(1)} %get-tuple-element.38.after_ref.refs_0_, bf16[8,32,128]{2,1,0:T(8,128)(2,1)S(1)} %collective-permute-done.refs_1_, bf16[8,32,128]{2,1,0:T(8,128)(2,1)S(1)} %collective-permute-done.1.refs_2_, ...), custom_call_target="tpu_custom_call" | custom-call | flops 2516582400 | bytes 19660800 | tf_op jit(solution)/shard_map/pallas_call | solution.py:409
  18.6 3.3 %shard_map.59 = (f32[608,128]{1,0:T(8,128)S(1)}, f32[608,128]{1,0:T(8,128)S(1)}, bf16[10,2,600,128]{3,2,1,0:T(8,128)(2,1)S(1)}) custom-call(bf16[8,32,128]{2,1,0:T(8,128)(2,1)S(1)} %get-tuple-element.38.after_ref.refs_0_, bf16[8,32,128]{2,1,0:T(8,128)(2,1)S(1)} %collective-permute-done.refs_1_, bf16[8,32,128]{2,1,0:T(8,128)(2,1)S(1)} %collective-permute-done.1.refs_2_, ...), custom_call_target="tpu_custom_call" | custom-call | flops 1258291200 | bytes 9830400 | tf_op jit(solution)/shard_map/pallas_call | solution.py:409
  22.6 1.1 %shard_map.60 = (f32[608,128]{1,0:T(8,128)S(1)}, f32[608,128]{1,0:T(8,128)S(1)}) custom-call(bf16[8,32,128]{2,1,0:T(8,128)(2,1)S(1)} %get-tuple-element.38.after_ref.refs_0_, bf16[8,32,128]{2,1,0:T(8,128)(2,1)S(1)} %collective-permute-done.refs_1_, bf16[8,32,128]{2,1,0:T(8,128)(2,1)S(1)} %collective-permute-done.1.refs_2_, ...), custom_call_target="tpu_custom_call" | custom-call | flops 393216000 | bytes 3072000 | tf_op jit(solution)/shard_map/pallas_call | solution.py:409
  23.8 2.9 %collective-permute-start.4 = (bf16[304,128]{1,0:T(8,128)(2,1)S(1)}, bf16[304,128]{1,0:T(8,128)(2,1)S(1)}, u32[]{:S(2)}, u32[]{:S(2)}) collective-permute-start(bf16[304,128]{1,0:T(8,128)(2,1)S(1)} %get-tuple-element.53), channel_id=1, source_target_pairs={{0,24},{8,16},{16,8},{24,0},{1,25},{9,17},{17,9},{25,1},{2,26},{10... | collective-permute-start | bytes 233480 | tf_op jit(solution)/shard_map/ppermute | solution.py:431
  27.5 2.9 %collective-permute-start.9 = (bf16[208,128]{1,0:T(8,128)(2,1)S(1)}, bf16[208,128]{1,0:T(8,128)(2,1)S(1)}, u32[]{:S(2)}, u32[]{:S(2)}) collective-permute-start(bf16[208,128]{1,0:T(8,128)(2,1)S(1)} %get-tuple-element.62), channel_id=1, source_target_pairs={{0,24},{8,16},{16,8},{24,0},{1,25},{9,17},{17,9},{25,1},{2,26},{10... | collective-permute-start | bytes 159752 | tf_op jit(solution)/shard_map/ppermute | solution.py:431
  30.9 0.6 %collective-permute-start.11 = (bf16[208,128]{1,0:T(8,128)(2,1)S(1)}, bf16[208,128]{1,0:T(8,128)(2,1)S(1)}, u32[]{:S(2)}, u32[]{:S(2)}) collective-permute-start(bf16[208,128]{1,0:T(8,128)(2,1)S(1)} %get-tuple-element.64), channel_id=1, source_target_pairs={{0,8},{8,0},{16,24},{24,16},{1,9},{9,1},{17,25},{25,17},{2,10},{10... | collective-permute-start | bytes 159752 | tf_op jit(solution)/shard_map/ppermute | solution.py:431
  31.5 0.6 %collective-permute-done.6.rest_3_ = bf16[304,128]{1,0:T(8,128)(2,1)S(1)} collective-permute-done((bf16[304,128]{1,0:T(8,128)(2,1)S(1)}, bf16[304,128]{1,0:T(8,128)(2,1)S(1)}, u32[]{:S(2)}, u32[]{:S(2)}) %collective-permute-start.6) | collective-permute-done | bytes 77856 | tf_op jit(solution)/shard_map/ppermute | solution.py:431
  32.1 1.3 %collective-permute-done.9.rest_5_ = bf16[208,128]{1,0:T(8,128)(2,1)S(1)} collective-permute-done((bf16[208,128]{1,0:T(8,128)(2,1)S(1)}, bf16[208,128]{1,0:T(8,128)(2,1)S(1)}, u32[]{:S(2)}, u32[]{:S(2)}) %collective-permute-start.9) | collective-permute-done | bytes 53280 | tf_op jit(solution)/shard_map/ppermute | solution.py:431
  33.5 1.1 %collective-permute-done.10.rest_6_ = bf16[208,128]{1,0:T(8,128)(2,1)S(1)} collective-permute-done((bf16[208,128]{1,0:T(8,128)(2,1)S(1)}, bf16[208,128]{1,0:T(8,128)(2,1)S(1)}, u32[]{:S(2)}, u32[]{:S(2)}) %collective-permute-start.10) | collective-permute-done | bytes 53280 | tf_op jit(solution)/shard_map/ppermute | solution.py:431
  35.0 1.4 %shard_map.62 = (f32[256,128]{1,0:T(8,128)S(1)}, bf16[256,128]{1,0:T(8,128)(2,1)S(1)}, bf16[256,128]{1,0:T(8,128)(2,1)S(1)}, bf16[256,128]{1,0:T(8,128)(2,1)S(1)}) custom-call(bf16[4,512,128]{2,1,0:T(8,128)(2,1)S(1)} %get-tuple-element.39.hits_ref, bf16[512,1024]{1,0:T(8,128)(2,1)S(1)} %copy-done.1, bf16[512,1024]{1,0:T(8,128)(2,1)S(1)} %copy-done, ...), custom_call_target="tpu_custom_call" | custom-call | tf_op jit(solution)/shard_map/pallas_call | solution.py:409
  36.4 3.7 %collective-permute-start.12 = (bf16[256,128]{1,0:T(8,128)(2,1)S(1)}, bf16[256,128]{1,0:T(8,128)(2,1)S(1)}, u32[]{:S(2)}, u32[]{:S(2)}) collective-permute-start(bf16[256,128]{1,0:T(8,128)(2,1)S(1)} %get-tuple-element.66), channel_id=1, source_target_pairs={{0,6},{1,7},{2,4},{3,5},{4,2},{5,3},{6,0},{7,1},{8,14},{9,15},{10,... | collective-permute-start | bytes 196616 | tf_op jit(solution)/shard_map/ppermute | solution.py:438
  40.1 0.8 %collective-permute-start.14 = (bf16[256,128]{1,0:T(8,128)(2,1)S(1)}, bf16[256,128]{1,0:T(8,128)(2,1)S(1)}, u32[]{:S(2)}, u32[]{:S(2)}) collective-permute-start(bf16[256,128]{1,0:T(8,128)(2,1)S(1)} %get-tuple-element.68), channel_id=1, source_target_pairs={{0,2},{1,3},{2,0},{3,1},{4,6},{5,7},{6,4},{7,5},{8,10},{9,11},{10,... | collective-permute-start | bytes 196616 | tf_op jit(solution)/shard_map/ppermute | solution.py:438
  40.9 1.7 %collective-permute-done.12.refs_1_ = bf16[256,128]{1,0:T(8,128)(2,1)S(1)} collective-permute-done((bf16[256,128]{1,0:T(8,128)(2,1)S(1)}, bf16[256,128]{1,0:T(8,128)(2,1)S(1)}, u32[]{:S(2)}, u32[]{:S(2)}) %collective-permute-start.12) | collective-permute-done | bytes 65568 | tf_op jit(solution)/shard_map/ppermute | solution.py:438
  42.6 2.7 %collective-permute-done.13.refs_2_ = bf16[256,128]{1,0:T(8,128)(2,1)S(1)} collective-permute-done((bf16[256,128]{1,0:T(8,128)(2,1)S(1)}, bf16[256,128]{1,0:T(8,128)(2,1)S(1)}, u32[]{:S(2)}, u32[]{:S(2)}) %collective-permute-start.13) | collective-permute-done | bytes 65568 | tf_op jit(solution)/shard_map/ppermute | solution.py:438
  45.3 2.1 %collective-permute-start.17 = (bf16[256,128]{1,0:T(8,128)(2,1)S(1)}, bf16[256,128]{1,0:T(8,128)(2,1)S(1)}, u32[]{:S(2)}, u32[]{:S(2)}) collective-permute-start(bf16[256,128]{1,0:T(8,128)(2,1)S(1)} %shard_map.63.refs_0_), channel_id=1, source_target_pairs={{0,6},{1,7},{2,4},{3,5},{4,2},{5,3},{6,0},{7,1},{8,14},{9,15},{10,... | collective-permute-start | bytes 196616 | tf_op jit(solution)/shard_map/ppermute | solution.py:438
  47.5 2.3 %collective-permute-start.15 = (bf16[256,128]{1,0:T(8,128)(2,1)S(1)}, bf16[256,128]{1,0:T(8,128)(2,1)S(1)}, u32[]{:S(2)}, u32[]{:S(2)}) collective-permute-start(bf16[256,128]{1,0:T(8,128)(2,1)S(1)} %shard_map.63.refs_0_), channel_id=1, source_target_pairs={{0,2},{1,3},{2,0},{3,1},{4,6},{5,7},{6,4},{7,5},{8,10},{9,11},{10,... | collective-permute-start | bytes 196616 | tf_op jit(solution)/shard_map/ppermute | solution.py:438
  49.8 1.7 %collective-permute-done.17.refs_3_ = bf16[256,128]{1,0:T(8,128)(2,1)S(1)} collective-permute-done((bf16[256,128]{1,0:T(8,128)(2,1)S(1)}, bf16[256,128]{1,0:T(8,128)(2,1)S(1)}, u32[]{:S(2)}, u32[]{:S(2)}) %collective-permute-start.17) | collective-permute-done | bytes 65568 | tf_op jit(solution)/shard_map/ppermute | solution.py:438
  51.4 1.8 %collective-permute-done.16.refs_2_ = bf16[256,128]{1,0:T(8,128)(2,1)S(1)} collective-permute-done((bf16[256,128]{1,0:T(8,128)(2,1)S(1)}, bf16[256,128]{1,0:T(8,128)(2,1)S(1)}, u32[]{:S(2)}, u32[]{:S(2)}) %collective-permute-start.16) | collective-permute-done | bytes 65568 | tf_op jit(solution)/shard_map/ppermute | solution.py:438
  53.7 1.1 %collective-permute-done.18.theirs_ref = bf16[1024,128]{1,0:T(8,128)(2,1)S(1)} collective-permute-done((bf16[1024,128]{1,0:T(8,128)(2,1)S(1)}, bf16[1024,128]{1,0:T(8,128)(2,1)S(1)}, u32[]{:S(2)}, u32[]{:S(2)}) %collective-permute-start.18) | collective-permute-done | bytes 262176 | tf_op jit(solution)/shard_map/ppermute | solution.py:441
  54.9 1.4 %shard_map.66 = f32[150,4,420]{2,1,0:T(4,128)} custom-call(f32[304,420]{1,0:T(8,128)S(1)} %get-tuple-element.69.mine_ref, bf16[1024,128]{1,0:T(8,128)(2,1)S(1)} %collective-permute-done.18.theirs_ref, bf16[420,512]{1,0:T(8,128)(2,1)S(1)} %get-tuple-element.70.pick_ref), custom_call_target="tpu_custom_call" | custom-call | tf_op jit(solution)/shard_map/pallas_call | solution.py:409
  (32 shorter events, 3.9 us)
Async XLA Ops:
  0.0 0.7 %copy-start.2 = (s32[424]{0:T(512)S(1)}, s32[424]{0:T(512)}, u32[]{:S(2)}) copy-start(s32[424]{0:T(512)} %param.7) | copy-start | bytes 5092
  3.5 9.3 %collective-permute-start = (bf16[8,32,128]{2,1,0:T(8,128)(2,1)S(1)}, bf16[8,32,128]{2,1,0:T(8,128)(2,1)S(1)}, u32[]{:S(2)}, u32[]{:S(2)}) collective-permute-start(bf16[8,32,128]{2,1,0:T(8,128)(2,1)S(1)} %get-tuple-element.40), channel_id=1, source_target_pairs={{0,24},{8,16},{16,8},{24,0},{1,25},{9,17},{17,9},{25,1},{2,26},{10... | collective-permute-start | bytes 196616 | tf_op jit(solution)/shard_map/ppermute | solution.py:431
  7.5 5.3 %collective-permute-start.1 = (bf16[8,32,128]{2,1,0:T(8,128)(2,1)S(1)}, bf16[8,32,128]{2,1,0:T(8,128)(2,1)S(1)}, u32[]{:S(2)}, u32[]{:S(2)}) collective-permute-start(bf16[8,32,128]{2,1,0:T(8,128)(2,1)S(1)} %get-tuple-element.41), channel_id=1, source_target_pairs={{0,16},{8,24},{16,0},{24,8},{1,17},{9,25},{17,1},{25,9},{2,18},{10... | collective-permute-start | bytes 196616 | tf_op jit(solution)/shard_map/ppermute | solution.py:431
  8.0 4.8 %collective-permute-start.2 = (bf16[8,32,128]{2,1,0:T(8,128)(2,1)S(1)}, bf16[8,32,128]{2,1,0:T(8,128)(2,1)S(1)}, u32[]{:S(2)}, u32[]{:S(2)}) collective-permute-start(bf16[8,32,128]{2,1,0:T(8,128)(2,1)S(1)} %get-tuple-element.42), channel_id=1, source_target_pairs={{0,8},{8,0},{16,24},{24,16},{1,9},{9,1},{17,25},{25,17},{2,10},{10... | collective-permute-start | bytes 196616 | tf_op jit(solution)/shard_map/ppermute | solution.py:431
  18.5 4.0 %collective-permute-start.3 = (f32[1216,128]{1,0:T(8,128)S(1)}, f32[1216,128]{1,0:T(8,128)S(1)}, u32[]{:S(2)}, u32[]{:S(2)}) collective-permute-start(f32[1216,128]{1,0:T(8,128)S(1)} %get-tuple-element.45), channel_id=1, source_target_pairs={{0,1},{1,0},{2,3},{3,2},{4,5},{5,4},{6,7},{7,6},{8,9},{9,8},{10,11... | collective-permute-start | bytes 1867784 | tf_op jit(solution)/shard_map/ppermute | solution.py:441
  21.9 13.1 %copy-start = (bf16[512,1024]{1,0:T(8,128)(2,1)S(1)}, bf16[512,1024]{1,0:T(8,128)(2,1)}, u32[]{:S(2)}) copy-start(bf16[512,1024]{1,0:T(8,128)(2,1)} %constant.5.clone.refs_3_.low_ref) | copy-start | bytes 3145732
  21.9 13.1 %copy-start.1 = (bf16[512,1024]{1,0:T(8,128)(2,1)S(1)}, bf16[512,1024]{1,0:T(8,128)(2,1)}, u32[]{:S(2)}) copy-start(bf16[512,1024]{1,0:T(8,128)(2,1)} %constant.4.clone.refs_2_.high_ref) | copy-start | bytes 3145732
  21.9 5.4 %collective-permute-start.7 = (f32[608,128]{1,0:T(8,128)S(1)}, f32[608,128]{1,0:T(8,128)S(1)}, u32[]{:S(2)}, u32[]{:S(2)}) collective-permute-start(f32[608,128]{1,0:T(8,128)S(1)} %get-tuple-element.57), channel_id=1, source_target_pairs={{0,1},{1,0},{2,3},{3,2},{4,5},{5,4},{6,7},{7,6},{8,9},{9,8},{10,11... | collective-permute-start | bytes 933896 | tf_op jit(solution)/shard_map/ppermute | solution.py:441
  23.7 3.6 %collective-permute-start.8 = (f32[608,128]{1,0:T(8,128)S(1)}, f32[608,128]{1,0:T(8,128)S(1)}, u32[]{:S(2)}, u32[]{:S(2)}) collective-permute-start(f32[608,128]{1,0:T(8,128)S(1)} %get-tuple-element.60), channel_id=1, source_target_pairs={{0,1},{1,0},{2,3},{3,2},{4,5},{5,4},{6,7},{7,6},{8,9},{9,8},{10,11... | collective-permute-start | bytes 933896 | tf_op jit(solution)/shard_map/ppermute | solution.py:441
  23.8 7.1 %collective-permute-start.4 = (bf16[304,128]{1,0:T(8,128)(2,1)S(1)}, bf16[304,128]{1,0:T(8,128)(2,1)S(1)}, u32[]{:S(2)}, u32[]{:S(2)}) collective-permute-start(bf16[304,128]{1,0:T(8,128)(2,1)S(1)} %get-tuple-element.53), channel_id=1, source_target_pairs={{0,24},{8,16},{16,8},{24,0},{1,25},{9,17},{17,9},{25,1},{2,26},{10... | collective-permute-start | bytes 233480 | tf_op jit(solution)/shard_map/ppermute | solution.py:431
  26.7 4.8 %collective-permute-start.5 = (bf16[304,128]{1,0:T(8,128)(2,1)S(1)}, bf16[304,128]{1,0:T(8,128)(2,1)S(1)}, u32[]{:S(2)}, u32[]{:S(2)}) collective-permute-start(bf16[304,128]{1,0:T(8,128)(2,1)S(1)} %get-tuple-element.54), channel_id=1, source_target_pairs={{0,16},{8,24},{16,0},{24,8},{1,17},{9,25},{17,1},{25,9},{2,18},{10... | collective-permute-start | bytes 233480 | tf_op jit(solution)/shard_map/ppermute | solution.py:431
  27.2 4.9 %collective-permute-start.6 = (bf16[304,128]{1,0:T(8,128)(2,1)S(1)}, bf16[304,128]{1,0:T(8,128)(2,1)S(1)}, u32[]{:S(2)}, u32[]{:S(2)}) collective-permute-start(bf16[304,128]{1,0:T(8,128)(2,1)S(1)} %get-tuple-element.55), channel_id=1, source_target_pairs={{0,8},{8,0},{16,24},{24,16},{1,9},{9,1},{17,25},{25,17},{2,10},{10... | collective-permute-start | bytes 233480 | tf_op jit(solution)/shard_map/ppermute | solution.py:431
  27.5 6.0 %collective-permute-start.9 = (bf16[208,128]{1,0:T(8,128)(2,1)S(1)}, bf16[208,128]{1,0:T(8,128)(2,1)S(1)}, u32[]{:S(2)}, u32[]{:S(2)}) collective-permute-start(bf16[208,128]{1,0:T(8,128)(2,1)S(1)} %get-tuple-element.62), channel_id=1, source_target_pairs={{0,24},{8,16},{16,8},{24,0},{1,25},{9,17},{17,9},{25,1},{2,26},{10... | collective-permute-start | bytes 159752 | tf_op jit(solution)/shard_map/ppermute | solution.py:431
  30.4 4.1 %collective-permute-start.10 = (bf16[208,128]{1,0:T(8,128)(2,1)S(1)}, bf16[208,128]{1,0:T(8,128)(2,1)S(1)}, u32[]{:S(2)}, u32[]{:S(2)}) collective-permute-start(bf16[208,128]{1,0:T(8,128)(2,1)S(1)} %get-tuple-element.63), channel_id=1, source_target_pairs={{0,16},{8,24},{16,0},{24,8},{1,17},{9,25},{17,1},{25,9},{2,18},{10... | collective-permute-start | bytes 159752 | tf_op jit(solution)/shard_map/ppermute | solution.py:431
  30.9 4.1 %collective-permute-start.11 = (bf16[208,128]{1,0:T(8,128)(2,1)S(1)}, bf16[208,128]{1,0:T(8,128)(2,1)S(1)}, u32[]{:S(2)}, u32[]{:S(2)}) collective-permute-start(bf16[208,128]{1,0:T(8,128)(2,1)S(1)} %get-tuple-element.64), channel_id=1, source_target_pairs={{0,8},{8,0},{16,24},{24,16},{1,9},{9,1},{17,25},{25,17},{2,10},{10... | collective-permute-start | bytes 159752 | tf_op jit(solution)/shard_map/ppermute | solution.py:431
  36.4 6.1 %collective-permute-start.12 = (bf16[256,128]{1,0:T(8,128)(2,1)S(1)}, bf16[256,128]{1,0:T(8,128)(2,1)S(1)}, u32[]{:S(2)}, u32[]{:S(2)}) collective-permute-start(bf16[256,128]{1,0:T(8,128)(2,1)S(1)} %get-tuple-element.66), channel_id=1, source_target_pairs={{0,6},{1,7},{2,4},{3,5},{4,2},{5,3},{6,0},{7,1},{8,14},{9,15},{10,... | collective-permute-start | bytes 196616 | tf_op jit(solution)/shard_map/ppermute | solution.py:438
  40.1 5.2 %collective-permute-start.13 = (bf16[256,128]{1,0:T(8,128)(2,1)S(1)}, bf16[256,128]{1,0:T(8,128)(2,1)S(1)}, u32[]{:S(2)}, u32[]{:S(2)}) collective-permute-start(bf16[256,128]{1,0:T(8,128)(2,1)S(1)} %get-tuple-element.67), channel_id=1, source_target_pairs={{0,4},{1,5},{2,6},{3,7},{4,0},{5,1},{6,2},{7,3},{8,12},{9,13},{10,... | collective-permute-start | bytes 196616 | tf_op jit(solution)/shard_map/ppermute | solution.py:438
  40.1 5.2 %collective-permute-start.14 = (bf16[256,128]{1,0:T(8,128)(2,1)S(1)}, bf16[256,128]{1,0:T(8,128)(2,1)S(1)}, u32[]{:S(2)}, u32[]{:S(2)}) collective-permute-start(bf16[256,128]{1,0:T(8,128)(2,1)S(1)} %get-tuple-element.68), channel_id=1, source_target_pairs={{0,2},{1,3},{2,0},{3,1},{4,6},{5,7},{6,4},{7,5},{8,10},{9,11},{10,... | collective-permute-start | bytes 196616 | tf_op jit(solution)/shard_map/ppermute | solution.py:438
  45.3 6.1 %collective-permute-start.17 = (bf16[256,128]{1,0:T(8,128)(2,1)S(1)}, bf16[256,128]{1,0:T(8,128)(2,1)S(1)}, u32[]{:S(2)}, u32[]{:S(2)}) collective-permute-start(bf16[256,128]{1,0:T(8,128)(2,1)S(1)} %shard_map.63.refs_0_), channel_id=1, source_target_pairs={{0,6},{1,7},{2,4},{3,5},{4,2},{5,3},{6,0},{7,1},{8,14},{9,15},{10,... | collective-permute-start | bytes 196616 | tf_op jit(solution)/shard_map/ppermute | solution.py:438
  47.4 5.9 %collective-permute-start.16 = (bf16[256,128]{1,0:T(8,128)(2,1)S(1)}, bf16[256,128]{1,0:T(8,128)(2,1)S(1)}, u32[]{:S(2)}, u32[]{:S(2)}) collective-permute-start(bf16[256,128]{1,0:T(8,128)(2,1)S(1)} %shard_map.63.refs_0_), channel_id=1, source_target_pairs={{0,4},{1,5},{2,6},{3,7},{4,0},{5,1},{6,2},{7,3},{8,12},{9,13},{10,... | collective-permute-start | bytes 196616 | tf_op jit(solution)/shard_map/ppermute | solution.py:438
  47.5 5.8 %collective-permute-start.15 = (bf16[256,128]{1,0:T(8,128)(2,1)S(1)}, bf16[256,128]{1,0:T(8,128)(2,1)S(1)}, u32[]{:S(2)}, u32[]{:S(2)}) collective-permute-start(bf16[256,128]{1,0:T(8,128)(2,1)S(1)} %shard_map.63.refs_0_), channel_id=1, source_target_pairs={{0,2},{1,3},{2,0},{3,1},{4,6},{5,7},{6,4},{7,5},{8,10},{9,11},{10,... | collective-permute-start | bytes 196616 | tf_op jit(solution)/shard_map/ppermute | solution.py:438
  53.3 1.6 %collective-permute-start.18 = (bf16[1024,128]{1,0:T(8,128)(2,1)S(1)}, bf16[1024,128]{1,0:T(8,128)(2,1)S(1)}, u32[]{:S(2)}, u32[]{:S(2)}) collective-permute-start(bf16[1024,128]{1,0:T(8,128)(2,1)S(1)} %shard_map.64.ref), channel_id=1, source_target_pairs={{0,1},{1,0},{2,3},{3,2},{4,5},{5,4},{6,7},{7,6},{8,9},{9,8},{10,11... | collective-permute-start | bytes 786440 | tf_op jit(solution)/shard_map/ppermute | solution.py:441

commit v4 on v3

--- a/solution.py
+++ b/solution.py
@@ -331,6 +331,8 @@
             value = jnp.zeros((pad, LANES), F32)
             for g, tile in enumerate(tiles):
                 inside = (lane // group == (g + comp) % plan.comps) & real_row
+                if g == plan.groups - 1:
+                    inside &= lane % group < plan.last
                 value = jnp.where(inside, tile, value)
             if comp:
                 value = pltpu.roll(value, LANES - comp * group, 1)

time: 56.4 us -> 56.5 us (level)
  no operation moved by 1% of the time
where the time goes in v4:
time: 56.5 us; the launch traced here: 56.3 us
  starting transfers between devices  21.9 us (39%)
  Pallas kernels  21.1 us (37%)
  waiting for transfers between devices  12.5 us (22%)
  local copies, waits for them, and re-layouts  0.69 us (1%)
    pallas_call x12, Pallas kernels, call(): pl.pallas_call(body, out_shape=out_shapes, in_specs=in_specs or [whole] *...  21.1 us
    ppermute x9, starting transfers between devices, over_freq(): lax.ppermute(values[k], 'freq', [(i, i ^ k) for i in range(freq)])  12.2 us
    ppermute x6, starting transfers between devices, to_piece(): return lax.ppermute(value, 'param', pairs)  8.91 us
    ppermute x6, waiting for transfers between devices, to_piece(): return lax.ppermute(value, 'param', pairs)  7.86 us
    ppermute x9, waiting for transfers between devices, over_freq(): lax.ppermute(values[k], 'freq', [(i, i ^ k) for i in range(freq)])  3.53 us
  transfers between devices with their start and end apart: 19, of which 9 were waited for; matrix products, arithmetic and copies ran while one was open for 0% of the time, Pallas kernels for 17%

profile of v4, /device:TPU:0, one launch (start us, length us, event | category | flops | bytes accessed | tf_op | source)
XLA Modules:
  0.0 56.3 jit_solution(5568585739387063595)
XLA Ops:
  0.0 0.7 %copy-done.2 = s32[424]{0:T(512)S(1)} copy-done((s32[424]{0:T(512)S(1)}, s32[424]{0:T(512)}, u32[]{:S(2)}) %copy-start.2) | copy-done | bytes 1720
  0.7 2.8 %shard_map.55 = (bf16[8,32,128]{2,1,0:T(8,128)(2,1)S(1)}, bf16[8,32,128]{2,1,0:T(8,128)(2,1)S(1)}, bf16[8,32,128]{2,1,0:T(8,128)(2,1)S(1)}, bf16[8,32,128]{2,1,0:T(8,128)(2,1)S(1)}) custom-call(s32[1,424]{1,0:T(1,128)S(1)} %bitcast.3, f32[4,32,420]{2,1,0:T(8,128)} %bitcast.5, bf16[512,1024]{1,0:T(8,128)(2,1)} %constant.4.clone.refs_2_.high_ref, ...), custom_call_target="tpu_custom_call" | custom-call | flops 2000000000 | bytes 1048576 | tf_op jit(solution)/shard_map/pallas_call | solution.py:411
  3.5 4.0 %collective-permute-start = (bf16[8,32,128]{2,1,0:T(8,128)(2,1)S(1)}, bf16[8,32,128]{2,1,0:T(8,128)(2,1)S(1)}, u32[]{:S(2)}, u32[]{:S(2)}) collective-permute-start(bf16[8,32,128]{2,1,0:T(8,128)(2,1)S(1)} %get-tuple-element.40), channel_id=1, source_target_pairs={{0,24},{8,16},{16,8},{24,0},{1,25},{9,17},{17,9},{25,1},{2,26},{10... | collective-permute-start | bytes 196616 | tf_op jit(solution)/shard_map/ppermute | solution.py:433
  8.1 4.6 %shard_map.56 = (bf16[40,2,600,128]{3,2,1,0:T(8,128)(2,1)S(1)}, bf16[4,512,128]{2,1,0:T(8,128)(2,1)S(1)}) custom-call(bf16[8,32,128]{2,1,0:T(8,128)(2,1)S(1)} %get-tuple-element.38.after_ref.refs_0_, s32[1,424]{1,0:T(1,128)S(1)} %bitcast.4, bf16[106,2,600,128]{3,2,1,0:T(8,128)(2,1)} %refs_5_.3), custom_call_target="tpu_custom_call" | custom-call | flops 4000000000 | bytes 12288000 | tf_op jit(solution)/shard_map/pallas_call | solution.py:411
  12.8 5.7 %shard_map.57 = (f32[1216,128]{1,0:T(8,128)S(1)}, f32[1216,128]{1,0:T(8,128)S(1)}, bf16[16,2,600,128]{3,2,1,0:T(8,128)(2,1)S(1)}) custom-call(bf16[8,32,128]{2,1,0:T(8,128)(2,1)S(1)} %get-tuple-element.38.after_ref.refs_0_, bf16[8,32,128]{2,1,0:T(8,128)(2,1)S(1)} %collective-permute-done.refs_1_, bf16[8,32,128]{2,1,0:T(8,128)(2,1)S(1)} %collective-permute-done.1.refs_2_, ...), custom_call_target="tpu_custom_call" | custom-call | flops 2516582400 | bytes 19660800 | tf_op jit(solution)/shard_map/pallas_call | solution.py:411
  18.6 3.3 %shard_map.59 = (f32[608,128]{1,0:T(8,128)S(1)}, f32[608,128]{1,0:T(8,128)S(1)}, bf16[10,2,600,128]{3,2,1,0:T(8,128)(2,1)S(1)}) custom-call(bf16[8,32,128]{2,1,0:T(8,128)(2,1)S(1)} %get-tuple-element.38.after_ref.refs_0_, bf16[8,32,128]{2,1,0:T(8,128)(2,1)S(1)} %collective-permute-done.refs_1_, bf16[8,32,128]{2,1,0:T(8,128)(2,1)S(1)} %collective-permute-done.1.refs_2_, ...), custom_call_target="tpu_custom_call" | custom-call | flops 1258291200 | bytes 9830400 | tf_op jit(solution)/shard_map/pallas_call | solution.py:411
  22.6 1.1 %shard_map.60 = (f32[608,128]{1,0:T(8,128)S(1)}, f32[608,128]{1,0:T(8,128)S(1)}) custom-call(bf16[8,32,128]{2,1,0:T(8,128)(2,1)S(1)} %get-tuple-element.38.after_ref.refs_0_, bf16[8,32,128]{2,1,0:T(8,128)(2,1)S(1)} %collective-permute-done.refs_1_, bf16[8,32,128]{2,1,0:T(8,128)(2,1)S(1)} %collective-permute-done.1.refs_2_, ...), custom_call_target="tpu_custom_call" | custom-call | flops 393216000 | bytes 3072000 | tf_op jit(solution)/shard_map/pallas_call | solution.py:411
  23.8 2.9 %collective-permute-start.4 = (bf16[304,128]{1,0:T(8,128)(2,1)S(1)}, bf16[304,128]{1,0:T(8,128)(2,1)S(1)}, u32[]{:S(2)}, u32[]{:S(2)}) collective-permute-start(bf16[304,128]{1,0:T(8,128)(2,1)S(1)} %get-tuple-element.53), channel_id=1, source_target_pairs={{0,24},{8,16},{16,8},{24,0},{1,25},{9,17},{17,9},{25,1},{2,26},{10... | collective-permute-start | bytes 233480 | tf_op jit(solution)/shard_map/ppermute | solution.py:433
  27.5 2.9 %collective-permute-start.9 = (bf16[208,128]{1,0:T(8,128)(2,1)S(1)}, bf16[208,128]{1,0:T(8,128)(2,1)S(1)}, u32[]{:S(2)}, u32[]{:S(2)}) collective-permute-start(bf16[208,128]{1,0:T(8,128)(2,1)S(1)} %get-tuple-element.62), channel_id=1, source_target_pairs={{0,24},{8,16},{16,8},{24,0},{1,25},{9,17},{17,9},{25,1},{2,26},{10... | collective-permute-start | bytes 159752 | tf_op jit(solution)/shard_map/ppermute | solution.py:433
  30.9 0.6 %collective-permute-start.11 = (bf16[208,128]{1,0:T(8,128)(2,1)S(1)}, bf16[208,128]{1,0:T(8,128)(2,1)S(1)}, u32[]{:S(2)}, u32[]{:S(2)}) collective-permute-start(bf16[208,128]{1,0:T(8,128)(2,1)S(1)} %get-tuple-element.64), channel_id=1, source_target_pairs={{0,8},{8,0},{16,24},{24,16},{1,9},{9,1},{17,25},{25,17},{2,10},{10... | collective-permute-start | bytes 159752 | tf_op jit(solution)/shard_map/ppermute | solution.py:433
  31.5 0.6 %collective-permute-done.6.rest_3_ = bf16[304,128]{1,0:T(8,128)(2,1)S(1)} collective-permute-done((bf16[304,128]{1,0:T(8,128)(2,1)S(1)}, bf16[304,128]{1,0:T(8,128)(2,1)S(1)}, u32[]{:S(2)}, u32[]{:S(2)}) %collective-permute-start.6) | collective-permute-done | bytes 77856 | tf_op jit(solution)/shard_map/ppermute | solution.py:433
  32.1 1.3 %collective-permute-done.9.rest_5_ = bf16[208,128]{1,0:T(8,128)(2,1)S(1)} collective-permute-done((bf16[208,128]{1,0:T(8,128)(2,1)S(1)}, bf16[208,128]{1,0:T(8,128)(2,1)S(1)}, u32[]{:S(2)}, u32[]{:S(2)}) %collective-permute-start.9) | collective-permute-done | bytes 53280 | tf_op jit(solution)/shard_map/ppermute | solution.py:433
  33.5 1.1 %collective-permute-done.10.rest_6_ = bf16[208,128]{1,0:T(8,128)(2,1)S(1)} collective-permute-done((bf16[208,128]{1,0:T(8,128)(2,1)S(1)}, bf16[208,128]{1,0:T(8,128)(2,1)S(1)}, u32[]{:S(2)}, u32[]{:S(2)}) %collective-permute-start.10) | collective-permute-done | bytes 53280 | tf_op jit(solution)/shard_map/ppermute | solution.py:433
  35.0 1.5 %shard_map.62 = (f32[256,128]{1,0:T(8,128)S(1)}, bf16[256,128]{1,0:T(8,128)(2,1)S(1)}, bf16[256,128]{1,0:T(8,128)(2,1)S(1)}, bf16[256,128]{1,0:T(8,128)(2,1)S(1)}) custom-call(bf16[4,512,128]{2,1,0:T(8,128)(2,1)S(1)} %get-tuple-element.39.hits_ref, bf16[512,1024]{1,0:T(8,128)(2,1)S(1)} %copy-done.1, bf16[512,1024]{1,0:T(8,128)(2,1)S(1)} %copy-done, ...), custom_call_target="tpu_custom_call" | custom-call | tf_op jit(solution)/shard_map/pallas_call | solution.py:411
  36.5 3.7 %collective-permute-start.12 = (bf16[256,128]{1,0:T(8,128)(2,1)S(1)}, bf16[256,128]{1,0:T(8,128)(2,1)S(1)}, u32[]{:S(2)}, u32[]{:S(2)}) collective-permute-start(bf16[256,128]{1,0:T(8,128)(2,1)S(1)} %get-tuple-element.66), channel_id=1, source_target_pairs={{0,6},{1,7},{2,4},{3,5},{4,2},{5,3},{6,0},{7,1},{8,14},{9,15},{10,... | collective-permute-start | bytes 196616 | tf_op jit(solution)/shard_map/ppermute | solution.py:440
  40.1 0.8 %collective-permute-start.14 = (bf16[256,128]{1,0:T(8,128)(2,1)S(1)}, bf16[256,128]{1,0:T(8,128)(2,1)S(1)}, u32[]{:S(2)}, u32[]{:S(2)}) collective-permute-start(bf16[256,128]{1,0:T(8,128)(2,1)S(1)} %get-tuple-element.68), channel_id=1, source_target_pairs={{0,2},{1,3},{2,0},{3,1},{4,6},{5,7},{6,4},{7,5},{8,10},{9,11},{10,... | collective-permute-start | bytes 196616 | tf_op jit(solution)/shard_map/ppermute | solution.py:440
  40.9 1.7 %collective-permute-done.12.refs_1_ = bf16[256,128]{1,0:T(8,128)(2,1)S(1)} collective-permute-done((bf16[256,128]{1,0:T(8,128)(2,1)S(1)}, bf16[256,128]{1,0:T(8,128)(2,1)S(1)}, u32[]{:S(2)}, u32[]{:S(2)}) %collective-permute-start.12) | collective-permute-done | bytes 65568 | tf_op jit(solution)/shard_map/ppermute | solution.py:440
  42.6 2.7 %collective-permute-done.13.refs_2_ = bf16[256,128]{1,0:T(8,128)(2,1)S(1)} collective-permute-done((bf16[256,128]{1,0:T(8,128)(2,1)S(1)}, bf16[256,128]{1,0:T(8,128)(2,1)S(1)}, u32[]{:S(2)}, u32[]{:S(2)}) %collective-permute-start.13) | collective-permute-done | bytes 65568 | tf_op jit(solution)/shard_map/ppermute | solution.py:440
  45.3 2.1 %collective-permute-start.17 = (bf16[256,128]{1,0:T(8,128)(2,1)S(1)}, bf16[256,128]{1,0:T(8,128)(2,1)S(1)}, u32[]{:S(2)}, u32[]{:S(2)}) collective-permute-start(bf16[256,128]{1,0:T(8,128)(2,1)S(1)} %shard_map.63.refs_0_), channel_id=1, source_target_pairs={{0,6},{1,7},{2,4},{3,5},{4,2},{5,3},{6,0},{7,1},{8,14},{9,15},{10,... | collective-permute-start | bytes 196616 | tf_op jit(solution)/shard_map/ppermute | solution.py:440
  47.5 2.3 %collective-permute-start.15 = (bf16[256,128]{1,0:T(8,128)(2,1)S(1)}, bf16[256,128]{1,0:T(8,128)(2,1)S(1)}, u32[]{:S(2)}, u32[]{:S(2)}) collective-permute-start(bf16[256,128]{1,0:T(8,128)(2,1)S(1)} %shard_map.63.refs_0_), channel_id=1, source_target_pairs={{0,2},{1,3},{2,0},{3,1},{4,6},{5,7},{6,4},{7,5},{8,10},{9,11},{10,... | collective-permute-start | bytes 196616 | tf_op jit(solution)/shard_map/ppermute | solution.py:440
  49.8 1.7 %collective-permute-done.17.refs_3_ = bf16[256,128]{1,0:T(8,128)(2,1)S(1)} collective-permute-done((bf16[256,128]{1,0:T(8,128)(2,1)S(1)}, bf16[256,128]{1,0:T(8,128)(2,1)S(1)}, u32[]{:S(2)}, u32[]{:S(2)}) %collective-permute-start.17) | collective-permute-done | bytes 65568 | tf_op jit(solution)/shard_map/ppermute | solution.py:440
  51.5 1.8 %collective-permute-done.16.refs_2_ = bf16[256,128]{1,0:T(8,128)(2,1)S(1)} collective-permute-done((bf16[256,128]{1,0:T(8,128)(2,1)S(1)}, bf16[256,128]{1,0:T(8,128)(2,1)S(1)}, u32[]{:S(2)}, u32[]{:S(2)}) %collective-permute-start.16) | collective-permute-done | bytes 65568 | tf_op jit(solution)/shard_map/ppermute | solution.py:440
  53.8 1.1 %collective-permute-done.18.theirs_ref = bf16[1024,128]{1,0:T(8,128)(2,1)S(1)} collective-permute-done((bf16[1024,128]{1,0:T(8,128)(2,1)S(1)}, bf16[1024,128]{1,0:T(8,128)(2,1)S(1)}, u32[]{:S(2)}, u32[]{:S(2)}) %collective-permute-start.18) | collective-permute-done | bytes 262176 | tf_op jit(solution)/shard_map/ppermute | solution.py:443
  54.9 1.4 %shard_map.66 = f32[150,4,420]{2,1,0:T(4,128)} custom-call(f32[304,420]{1,0:T(8,128)S(1)} %get-tuple-element.69.mine_ref, bf16[1024,128]{1,0:T(8,128)(2,1)S(1)} %collective-permute-done.18.theirs_ref, bf16[420,512]{1,0:T(8,128)(2,1)S(1)} %get-tuple-element.70.pick_ref), custom_call_target="tpu_custom_call" | custom-call | tf_op jit(solution)/shard_map/pallas_call | solution.py:411
  (32 shorter events, 3.9 us)
Async XLA Ops:
  0.0 0.7 %copy-start.2 = (s32[424]{0:T(512)S(1)}, s32[424]{0:T(512)}, u32[]{:S(2)}) copy-start(s32[424]{0:T(512)} %param.7) | copy-start | bytes 5092
  3.5 9.3 %collective-permute-start = (bf16[8,32,128]{2,1,0:T(8,128)(2,1)S(1)}, bf16[8,32,128]{2,1,0:T(8,128)(2,1)S(1)}, u32[]{:S(2)}, u32[]{:S(2)}) collective-permute-start(bf16[8,32,128]{2,1,0:T(8,128)(2,1)S(1)} %get-tuple-element.40), channel_id=1, source_target_pairs={{0,24},{8,16},{16,8},{24,0},{1,25},{9,17},{17,9},{25,1},{2,26},{10... | collective-permute-start | bytes 196616 | tf_op jit(solution)/shard_map/ppermute | solution.py:433
  7.5 5.3 %collective-permute-start.1 = (bf16[8,32,128]{2,1,0:T(8,128)(2,1)S(1)}, bf16[8,32,128]{2,1,0:T(8,128)(2,1)S(1)}, u32[]{:S(2)}, u32[]{:S(2)}) collective-permute-start(bf16[8,32,128]{2,1,0:T(8,128)(2,1)S(1)} %get-tuple-element.41), channel_id=1, source_target_pairs={{0,16},{8,24},{16,0},{24,8},{1,17},{9,25},{17,1},{25,9},{2,18},{10... | collective-permute-start | bytes 196616 | tf_op jit(solution)/shard_map/ppermute | solution.py:433
  8.0 4.8 %collective-permute-start.2 = (bf16[8,32,128]{2,1,0:T(8,128)(2,1)S(1)}, bf16[8,32,128]{2,1,0:T(8,128)(2,1)S(1)}, u32[]{:S(2)}, u32[]{:S(2)}) collective-permute-start(bf16[8,32,128]{2,1,0:T(8,128)(2,1)S(1)} %get-tuple-element.42), channel_id=1, source_target_pairs={{0,8},{8,0},{16,24},{24,16},{1,9},{9,1},{17,25},{25,17},{2,10},{10... | collective-permute-start | bytes 196616 | tf_op jit(solution)/shard_map/ppermute | solution.py:433
  18.5 4.0 %collective-permute-start.3 = (f32[1216,128]{1,0:T(8,128)S(1)}, f32[1216,128]{1,0:T(8,128)S(1)}, u32[]{:S(2)}, u32[]{:S(2)}) collective-permute-start(f32[1216,128]{1,0:T(8,128)S(1)} %get-tuple-element.45), channel_id=1, source_target_pairs={{0,1},{1,0},{2,3},{3,2},{4,5},{5,4},{6,7},{7,6},{8,9},{9,8},{10,11... | collective-permute-start | bytes 1867784 | tf_op jit(solution)/shard_map/ppermute | solution.py:443
  21.9 13.1 %copy-start = (bf16[512,1024]{1,0:T(8,128)(2,1)S(1)}, bf16[512,1024]{1,0:T(8,128)(2,1)}, u32[]{:S(2)}) copy-start(bf16[512,1024]{1,0:T(8,128)(2,1)} %constant.5.clone.refs_3_.low_ref) | copy-start | bytes 3145732
  21.9 13.1 %copy-start.1 = (bf16[512,1024]{1,0:T(8,128)(2,1)S(1)}, bf16[512,1024]{1,0:T(8,128)(2,1)}, u32[]{:S(2)}) copy-start(bf16[512,1024]{1,0:T(8,128)(2,1)} %constant.4.clone.refs_2_.high_ref) | copy-start | bytes 3145732
  21.9 5.4 %collective-permute-start.7 = (f32[608,128]{1,0:T(8,128)S(1)}, f32[608,128]{1,0:T(8,128)S(1)}, u32[]{:S(2)}, u32[]{:S(2)}) collective-permute-start(f32[608,128]{1,0:T(8,128)S(1)} %get-tuple-element.57), channel_id=1, source_target_pairs={{0,1},{1,0},{2,3},{3,2},{4,5},{5,4},{6,7},{7,6},{8,9},{9,8},{10,11... | collective-permute-start | bytes 933896 | tf_op jit(solution)/shard_map/ppermute | solution.py:443
  23.7 3.6 %collective-permute-start.8 = (f32[608,128]{1,0:T(8,128)S(1)}, f32[608,128]{1,0:T(8,128)S(1)}, u32[]{:S(2)}, u32[]{:S(2)}) collective-permute-start(f32[608,128]{1,0:T(8,128)S(1)} %get-tuple-element.60), channel_id=1, source_target_pairs={{0,1},{1,0},{2,3},{3,2},{4,5},{5,4},{6,7},{7,6},{8,9},{9,8},{10,11... | collective-permute-start | bytes 933896 | tf_op jit(solution)/shard_map/ppermute | solution.py:443
  23.8 7.1 %collective-permute-start.4 = (bf16[304,128]{1,0:T(8,128)(2,1)S(1)}, bf16[304,128]{1,0:T(8,128)(2,1)S(1)}, u32[]{:S(2)}, u32[]{:S(2)}) collective-permute-start(bf16[304,128]{1,0:T(8,128)(2,1)S(1)} %get-tuple-element.53), channel_id=1, source_target_pairs={{0,24},{8,16},{16,8},{24,0},{1,25},{9,17},{17,9},{25,1},{2,26},{10... | collective-permute-start | bytes 233480 | tf_op jit(solution)/shard_map/ppermute | solution.py:433
  26.7 4.8 %collective-permute-start.5 = (bf16[304,128]{1,0:T(8,128)(2,1)S(1)}, bf16[304,128]{1,0:T(8,128)(2,1)S(1)}, u32[]{:S(2)}, u32[]{:S(2)}) collective-permute-start(bf16[304,128]{1,0:T(8,128)(2,1)S(1)} %get-tuple-element.54), channel_id=1, source_target_pairs={{0,16},{8,24},{16,0},{24,8},{1,17},{9,25},{17,1},{25,9},{2,18},{10... | collective-permute-start | bytes 233480 | tf_op jit(solution)/shard_map/ppermute | solution.py:433
  27.2 4.9 %collective-permute-start.6 = (bf16[304,128]{1,0:T(8,128)(2,1)S(1)}, bf16[304,128]{1,0:T(8,128)(2,1)S(1)}, u32[]{:S(2)}, u32[]{:S(2)}) collective-permute-start(bf16[304,128]{1,0:T(8,128)(2,1)S(1)} %get-tuple-element.55), channel_id=1, source_target_pairs={{0,8},{8,0},{16,24},{24,16},{1,9},{9,1},{17,25},{25,17},{2,10},{10... | collective-permute-start | bytes 233480 | tf_op jit(solution)/shard_map/ppermute | solution.py:433
  27.5 6.0 %collective-permute-start.9 = (bf16[208,128]{1,0:T(8,128)(2,1)S(1)}, bf16[208,128]{1,0:T(8,128)(2,1)S(1)}, u32[]{:S(2)}, u32[]{:S(2)}) collective-permute-start(bf16[208,128]{1,0:T(8,128)(2,1)S(1)} %get-tuple-element.62), channel_id=1, source_target_pairs={{0,24},{8,16},{16,8},{24,0},{1,25},{9,17},{17,9},{25,1},{2,26},{10... | collective-permute-start | bytes 159752 | tf_op jit(solution)/shard_map/ppermute | solution.py:433
  30.4 4.1 %collective-permute-start.10 = (bf16[208,128]{1,0:T(8,128)(2,1)S(1)}, bf16[208,128]{1,0:T(8,128)(2,1)S(1)}, u32[]{:S(2)}, u32[]{:S(2)}) collective-permute-start(bf16[208,128]{1,0:T(8,128)(2,1)S(1)} %get-tuple-element.63), channel_id=1, source_target_pairs={{0,16},{8,24},{16,0},{24,8},{1,17},{9,25},{17,1},{25,9},{2,18},{10... | collective-permute-start | bytes 159752 | tf_op jit(solution)/shard_map/ppermute | solution.py:433
  30.9 4.1 %collective-permute-start.11 = (bf16[208,128]{1,0:T(8,128)(2,1)S(1)}, bf16[208,128]{1,0:T(8,128)(2,1)S(1)}, u32[]{:S(2)}, u32[]{:S(2)}) collective-permute-start(bf16[208,128]{1,0:T(8,128)(2,1)S(1)} %get-tuple-element.64), channel_id=1, source_target_pairs={{0,8},{8,0},{16,24},{24,16},{1,9},{9,1},{17,25},{25,17},{2,10},{10... | collective-permute-start | bytes 159752 | tf_op jit(solution)/shard_map/ppermute | solution.py:433
  36.5 6.1 %collective-permute-start.12 = (bf16[256,128]{1,0:T(8,128)(2,1)S(1)}, bf16[256,128]{1,0:T(8,128)(2,1)S(1)}, u32[]{:S(2)}, u32[]{:S(2)}) collective-permute-start(bf16[256,128]{1,0:T(8,128)(2,1)S(1)} %get-tuple-element.66), channel_id=1, source_target_pairs={{0,6},{1,7},{2,4},{3,5},{4,2},{5,3},{6,0},{7,1},{8,14},{9,15},{10,... | collective-permute-start | bytes 196616 | tf_op jit(solution)/shard_map/ppermute | solution.py:440
  40.1 5.2 %collective-permute-start.13 = (bf16[256,128]{1,0:T(8,128)(2,1)S(1)}, bf16[256,128]{1,0:T(8,128)(2,1)S(1)}, u32[]{:S(2)}, u32[]{:S(2)}) collective-permute-start(bf16[256,128]{1,0:T(8,128)(2,1)S(1)} %get-tuple-element.67), channel_id=1, source_target_pairs={{0,4},{1,5},{2,6},{3,7},{4,0},{5,1},{6,2},{7,3},{8,12},{9,13},{10,... | collective-permute-start | bytes 196616 | tf_op jit(solution)/shard_map/ppermute | solution.py:440
  40.1 5.2 %collective-permute-start.14 = (bf16[256,128]{1,0:T(8,128)(2,1)S(1)}, bf16[256,128]{1,0:T(8,128)(2,1)S(1)}, u32[]{:S(2)}, u32[]{:S(2)}) collective-permute-start(bf16[256,128]{1,0:T(8,128)(2,1)S(1)} %get-tuple-element.68), channel_id=1, source_target_pairs={{0,2},{1,3},{2,0},{3,1},{4,6},{5,7},{6,4},{7,5},{8,10},{9,11},{10,... | collective-permute-start | bytes 196616 | tf_op jit(solution)/shard_map/ppermute | solution.py:440
  45.3 6.1 %collective-permute-start.17 = (bf16[256,128]{1,0:T(8,128)(2,1)S(1)}, bf16[256,128]{1,0:T(8,128)(2,1)S(1)}, u32[]{:S(2)}, u32[]{:S(2)}) collective-permute-start(bf16[256,128]{1,0:T(8,128)(2,1)S(1)} %shard_map.63.refs_0_), channel_id=1, source_target_pairs={{0,6},{1,7},{2,4},{3,5},{4,2},{5,3},{6,0},{7,1},{8,14},{9,15},{10,... | collective-permute-start | bytes 196616 | tf_op jit(solution)/shard_map/ppermute | solution.py:440
  47.4 5.9 %collective-permute-start.16 = (bf16[256,128]{1,0:T(8,128)(2,1)S(1)}, bf16[256,128]{1,0:T(8,128)(2,1)S(1)}, u32[]{:S(2)}, u32[]{:S(2)}) collective-permute-start(bf16[256,128]{1,0:T(8,128)(2,1)S(1)} %shard_map.63.refs_0_), channel_id=1, source_target_pairs={{0,4},{1,5},{2,6},{3,7},{4,0},{5,1},{6,2},{7,3},{8,12},{9,13},{10,... | collective-permute-start | bytes 196616 | tf_op jit(solution)/shard_map/ppermute | solution.py:440
  47.5 5.8 %collective-permute-start.15 = (bf16[256,128]{1,0:T(8,128)(2,1)S(1)}, bf16[256,128]{1,0:T(8,128)(2,1)S(1)}, u32[]{:S(2)}, u32[]{:S(2)}) collective-permute-start(bf16[256,128]{1,0:T(8,128)(2,1)S(1)} %shard_map.63.refs_0_), channel_id=1, source_target_pairs={{0,2},{1,3},{2,0},{3,1},{4,6},{5,7},{6,4},{7,5},{8,10},{9,11},{10,... | collective-permute-start | bytes 196616 | tf_op jit(solution)/shard_map/ppermute | solution.py:440
  53.3 1.6 %collective-permute-start.18 = (bf16[1024,128]{1,0:T(8,128)(2,1)S(1)}, bf16[1024,128]{1,0:T(8,128)(2,1)S(1)}, u32[]{:S(2)}, u32[]{:S(2)}) collective-permute-start(bf16[1024,128]{1,0:T(8,128)(2,1)S(1)} %shard_map.64.ref), channel_id=1, source_target_pairs={{0,1},{1,0},{2,3},{3,2},{4,5},{5,4},{6,7},{7,6},{8,9},{9,8},{10,11... | collective-permute-start | bytes 786440 | tf_op jit(solution)/shard_map/ppermute | solution.py:443
